TPU v7x, 1024 devices: a whole 4x4x32 slice. The times are simulated.
1024 devices in a mesh: gx: 256 (over y, z, core), gy: 4 (over x).
Axes of the slice: x: 4, y: 4, z: 32, core: 2. Of those that a mesh axis runs over, the one named last changes fastest.
Arguments:
- forcing: float32 [2048, 32, 128], P('gx', 'gy'), may hold values from -12 to 12
- kappa: float32 [256, 4, 16], P('gx', 'gy'), may hold values from 0.25 to 4
- sigma: float32 [256, 4, 16], P('gx', 'gy'), may hold values from 0.5 to 8
Outputs:
- solution: float32 [2048, 32, 128], P('gx', 'gy')
- residual: float32 [2048, 32, 128], P('gx', 'gy')
- rel_residual: float32 [], replicated
All inputs are finite; a program needn't handle non-finite values.
Results may differ from a plain program's by a relative error of at most 0.0003.
Values sent between devices are 32-bit elements; how exact they have to be, the bound alone decides.
A program may use at most 64 MiB of HBM per device.

v0:
```python
import functools

import jax
import jax.numpy as jnp
import numpy as np
from jax import lax
from jax.sharding import Mesh
from jax.sharding import PartitionSpec as P

GX = ("gx_0", "gx_1", "gx_2")
GX_GY = ("gx_0", "gx_1", "gx_2", "gy")


def with_halo(cells, sides, width):
    for axis, dim in sides:
        count = lax.axis_size(axis)
        head = lax.slice_in_dim(cells, 0, width, axis=dim)
        tail = lax.slice_in_dim(cells, cells.shape[dim] - width, cells.shape[dim], axis=dim)
        cells = jnp.concatenate(
            [
                lax.ppermute(tail, axis, [(i, (i + 1) % count) for i in range(count)]),
                cells,
                lax.ppermute(head, axis, [((i + 1) % count, i) for i in range(count)]),
            ],
            axis=dim,
        )
    return cells


def one_axis_at_a_time(shard, axes):
    return functools.reduce(lax.psum, axes, shard)


def legendre_table(points, order):
    columns = [points * 0.0 + 1.0, points]
    for degree in range(2, order + 1):
        columns.append(
            ((2 * degree - 1) * points * columns[-1] - (degree - 1) * columns[-2]) / degree
        )
    return np.stack(columns, axis=1)


def lobatto(count):
    order = count - 1
    points = np.cos(np.pi * np.arange(count) / order)
    for sweep in range(60):
        table = legendre_table(points, order)
        points = points - (points * table[:, order] - table[:, order - 1]) / (
            count * table[:, order]
        )
    table = legendre_table(points, order)
    weights = 2.0 / (order * count * table[:, order] ** 2)
    values = table[:, order]
    points, weights, values = (points[::-1], weights[::-1], values[::-1])
    spread = points[:, None] - points[None, :] + np.eye(count)
    deriv = values[:, None] / values[None, :] / spread * (1.0 - np.eye(count))
    corner = order * (order + 1) / 4.0
    ends = np.array([-corner] + [0.0] * (count - 2) + [corner])
    return (points, weights, deriv + np.eye(count) * ends[None, :])


def lagrange(fine_points, coarse_points):
    columns = []
    for column in range(len(coarse_points)):
        value = fine_points * 0.0 + 1.0
        for other in range(len(coarse_points)):
            if other != column:
                value = (
                    value
                    * (fine_points - coarse_points[other])
                    / (coarse_points[column] - coarse_points[other])
                )
        columns.append(value)
    return np.stack(columns, axis=1)


def edge_factor(count, blocks):
    index = jnp.arange(count)
    single = jnp.where((index == 0) | (index == count - 1), 0.5, 1.0).astype(jnp.float32)
    return jnp.tile(single, blocks)


def multiplicity(count, blocks):
    first = edge_factor(count, blocks[0])
    second = edge_factor(count, blocks[1])
    third = edge_factor(count, blocks[2])
    return first[:, None, None] * second[None, :, None] * third[None, None, :]


def element_apply(field, kappa, sigma, deriv, weights):
    count = deriv.shape[0]
    ex, ey, ez = kappa.shape
    high = lax.Precision.HIGHEST
    block = field.reshape(ex, count, ey, count, ez, count)
    mass = (weights[:, None, None] * weights[None, :, None] * weights[None, None, :])[
        None, :, None, :, None, :
    ]
    first = jnp.einsum("ai,eifjgk->eafjgk", deriv, block, precision=high)
    total = jnp.einsum("ai,eafjgk->eifjgk", deriv, first * mass, precision=high)
    second = jnp.einsum("aj,eifjgk->eifagk", deriv, block, precision=high)
    total = total + jnp.einsum("aj,eifagk->eifjgk", deriv, second * mass, precision=high)
    third = jnp.einsum("ak,eifjgk->eifjga", deriv, block, precision=high)
    total = total + jnp.einsum("ak,eifjga->eifjgk", deriv, third * mass, precision=high)
    coeff = kappa[:, None, :, None, :, None]
    shift = sigma[:, None, :, None, :, None]
    return (coeff * total + shift * mass * block).reshape(field.shape)


def element_diagonal(kappa, sigma, deriv, weights):
    count = deriv.shape[0]
    ex, ey, ez = kappa.shape
    stiff = jnp.sum(deriv * deriv * weights[:, None], axis=0)
    term = stiff[:, None, None] * weights[None, :, None] * weights[None, None, :]
    term = term + weights[:, None, None] * stiff[None, :, None] * weights[None, None, :]
    term = term + weights[:, None, None] * weights[None, :, None] * stiff[None, None, :]
    mass = weights[:, None, None] * weights[None, :, None] * weights[None, None, :]
    coeff = kappa[:, None, :, None, :, None]
    shift = sigma[:, None, :, None, :, None]
    full = coeff * term[None, :, None, :, None, :] + shift * mass[None, :, None, :, None, :]
    return full.reshape(ex * count, ey * count, ez * count)


def fold_axis(field, dim, count):
    size = field.shape[dim]
    position = jnp.arange(size) % count
    shape = [1, 1, 1]
    shape[dim] = size
    first = (position == 0).reshape(shape)
    last = (position == count - 1).reshape(shape)
    before = jnp.roll(field, 1, dim)
    after = jnp.roll(field, -1, dim)
    return field + jnp.where(first, before, 0.0) + jnp.where(last, after, 0.0)


def fold_padded(padded, dim, count):
    size = padded.shape[dim] - 2
    center = lax.slice_in_dim(padded, 1, size + 1, axis=dim)
    before = lax.slice_in_dim(padded, 0, size, axis=dim)
    after = lax.slice_in_dim(padded, 2, size + 2, axis=dim)
    position = jnp.arange(size) % count
    shape = [1, 1, 1]
    shape[dim] = size
    first = (position == 0).reshape(shape)
    last = (position == count - 1).reshape(shape)
    return center + jnp.where(first, before, 0.0) + jnp.where(last, after, 0.0)


def assemble(field, count, finest):
    if finest:
        rows = with_halo(field, ((GX, 0),), 1)
        field = fold_padded(rows, 0, count)
        columns = with_halo(field, (("gy", 1),), 1)
        field = fold_padded(columns, 1, count)
    else:
        padded = with_halo(field, ((GX, 0), ("gy", 1)), 1)
        field = fold_padded(fold_padded(padded, 0, count), 1, count)
    return fold_axis(field, 2, count)


def restrict(field, interp, blocks, fine_count, coarse_count):
    high = lax.Precision.HIGHEST
    block = field.reshape(blocks[0], fine_count, blocks[1], fine_count, blocks[2], fine_count)
    one = jnp.einsum("ia,eifjgk->eafjgk", interp, block, precision=high)
    two = jnp.einsum("jb,eafjgk->eafbgk", interp, one, precision=high)
    three = jnp.einsum("kc,eafbgk->eafbgc", interp, two, precision=high)
    return three.reshape(
        blocks[0] * coarse_count, blocks[1] * coarse_count, blocks[2] * coarse_count
    )


def prolong(field, interp, blocks, fine_count, coarse_count):
    high = lax.Precision.HIGHEST
    block = field.reshape(blocks[0], coarse_count, blocks[1], coarse_count, blocks[2], coarse_count)
    one = jnp.einsum("ia,eafbgc->eifbgc", interp, block, precision=high)
    two = jnp.einsum("jb,eifbgc->eifjgc", interp, one, precision=high)
    three = jnp.einsum("kc,eifjgc->eifjgk", interp, two, precision=high)
    return three.reshape(blocks[0] * fine_count, blocks[1] * fine_count, blocks[2] * fine_count)


def local(forcing, kappa, sigma):
    blocks = kappa.shape
    counts = [8, 4, 2]
    tables = [lobatto(count) for count in counts]
    derivs = [jnp.asarray(table[2], jnp.float32) for table in tables]
    weights = [jnp.asarray(table[1], jnp.float32) for table in tables]
    interps = [
        jnp.asarray(lagrange(tables[level][0], tables[level + 1][0]), jnp.float32)
        for level in range(2)
    ]
    mults = [multiplicity(count, blocks) for count in counts]
    diags = [
        assemble(
            element_diagonal(kappa, sigma, derivs[level], weights[level]), counts[level], level == 0
        )
        for level in range(3)
    ]
    center = 1.65
    half = 1.35
    ratio = center / half

    def operate(field, level):
        return assemble(
            element_apply(field, kappa, sigma, derivs[level], weights[level]),
            counts[level],
            level == 0,
        )

    def smooth(resid, level, steps, keep_last):
        rho = 1.0 / ratio
        direction = resid / (center * diags[level])
        iterate = direction
        for step in range(steps):
            if step > 0:
                rho_next = 1.0 / (2.0 * ratio - rho)
                direction = (
                    rho_next * rho * direction + 2.0 * rho_next / half * resid / diags[level]
                )
                iterate = iterate + direction
                rho = rho_next
            if step < steps - 1 or keep_last:
                resid = resid - operate(direction, level)
        return (iterate, resid)

    def vcycle(resid, level):
        if level == 2:
            iterate, unused = smooth(resid, level, 2, False)
            return iterate
        iterate, resid = smooth(resid, level, 2, True)
        coarse = assemble(
            restrict(
                mults[level] * resid, interps[level], blocks, counts[level], counts[level + 1]
            ),
            counts[level + 1],
            False,
        )
        correction = prolong(
            vcycle(coarse, level + 1), interps[level], blocks, counts[level], counts[level + 1]
        )
        iterate = iterate + correction
        resid = resid - operate(correction, level)
        return iterate + resid / (center * diags[level])

    load = assemble(forcing, 8, True)
    first = vcycle(load, 0)
    image_first = operate(first, 0)
    second = vcycle(load - image_first, 0)
    combined = first + second
    image = operate(combined, 0)
    weight = mults[0]
    load_sq, load_image, image_sq = (
        one_axis_at_a_time(jnp.sum(weight * load * load), GX_GY),
        one_axis_at_a_time(jnp.sum(weight * load * image), GX_GY),
        one_axis_at_a_time(jnp.sum(weight * image * image), GX_GY),
    )
    coef = load_image / image_sq
    solution = coef * combined
    residual = load - coef * image
    rel_residual = jnp.sqrt((load_sq - load_image * load_image / image_sq) / load_sq)
    return (solution, residual, rel_residual)


def solution(mesh):
    split = Mesh(mesh.devices.reshape(4, 32, 2, mesh.shape["gy"]), ("gx_0", "gx_1", "gx_2", "gy"))
    return jax.shard_map(
        local,
        mesh=split,
        in_specs=(P(GX, "gy", None), P(GX, "gy", None), P(GX, "gy", None)),
        out_specs=(P(GX, "gy", None), P(GX, "gy", None), P()),
        check_vma=False,
    )
```

profile of v0, /device:TPU:1, one launch (start us, length us, event | category | flops | bytes accessed | tf_op | source)
XLA Modules:
  0.0 642.9 jit_solution(10439646342837640624)
XLA Ops:
  1.3 5.0 collective-permute-start
  6.4 13.0 %collective-permute-start.1 = (f32[1,8,128]{2,1,0:T(8,128)S(1)}, f32[1,8,128]{2,1,0:T(8,128)S(1)}, u32[]{:S(2)}, u32[]{:S(2)}) collective-permute-start(f32[1,8,128]{2,1,0:T(8,128)S(1)} %get-tuple-element.141), channel_id=1, source_target_pairs={{4,0},{8,4},{12,8},{16,12},{20,16},{24,20},{28,24},{32,28},{36,32}... | collective-permute-start | bytes 12296 | tf_op jit(solution)/shard_map/ppermute | solution.py:23
  19.6 7.9 %collective-permute-start.37 = (f32[1,2,32]{2,1,0:T(2,128)S(1)}, f32[1,2,32]{2,1,0:T(2,128)S(1)}, u32[]{:S(2)}, u32[]{:S(2)}) collective-permute-start(f32[1,2,32]{2,1,0:T(2,128)S(1)} %slice.1273), channel_id=1, source_target_pairs={{4,0},{8,4},{12,8},{16,12},{20,16},{24,20},{28,24},{32,28},{36,32}... | collective-permute-start | bytes 776 | tf_op jit(solution)/shard_map/ppermute | solution.py:23
  36.1 3.1 collective-permute-start.2
  39.2 3.4 collective-permute-start.3
  42.8 3.5 collective-permute-start.36
  50.3 4.6 collective-permute-start.7
  57.4 3.7 fusion.527
  67.6 5.9 collective-permute-start.9
  76.9 4.9 collective-permute-start.11
  82.8 3.7 fusion.529
  92.6 8.3 %collective-permute-start.13 = (f32[1,8,128]{2,1,0:T(8,128)S(1)}, f32[1,8,128]{2,1,0:T(8,128)S(1)}, u32[]{:S(2)}, u32[]{:S(2)}) collective-permute-start(f32[1,8,128]{2,1,0:T(8,128)S(1)} %slice.1182), channel_id=1, source_target_pairs={{4,0},{8,4},{12,8},{16,12},{20,16},{24,20},{28,24},{32,28},{36,32}... | collective-permute-start | bytes 12296 | tf_op jit(solution)/shard_map/ppermute | solution.py:23
  101.9 3.3 collective-permute-start.14
  105.2 3.7 collective-permute-start.15
  109.2 7.7 %collective-permute-start.21 = (f32[1,4,64]{2,1,0:T(4,128)S(1)}, f32[1,4,64]{2,1,0:T(4,128)S(1)}, u32[]{:S(2)}, u32[]{:S(2)}) collective-permute-start(f32[1,4,64]{2,1,0:T(4,128)S(1)} %slice.1211), channel_id=1, source_target_pairs={{4,0},{8,4},{12,8},{16,12},{20,16},{24,20},{28,24},{32,28},{36,32}... | collective-permute-start | bytes 3080 | tf_op jit(solution)/shard_map/ppermute | solution.py:23
  123.3 4.6 collective-permute-start.23
  128.4 7.2 %collective-permute-start.17 = (f32[1,4,64]{2,1,0:T(4,128)S(1)}, f32[1,4,64]{2,1,0:T(4,128)S(1)}, u32[]{:S(2)}, u32[]{:S(2)}) collective-permute-start(f32[1,4,64]{2,1,0:T(4,128)S(1)} %slice.1195), channel_id=1, source_target_pairs={{4,0},{8,4},{12,8},{16,12},{20,16},{24,20},{28,24},{32,28},{36,32}... | collective-permute-start | bytes 3080 | tf_op jit(solution)/shard_map/ppermute | solution.py:23
  138.3 4.6 collective-permute-start.19
  150.4 8.0 %collective-permute-start.25 = (f32[1,4,64]{2,1,0:T(4,128)S(1)}, f32[1,4,64]{2,1,0:T(4,128)S(1)}, u32[]{:S(2)}, u32[]{:S(2)}) collective-permute-start(f32[1,4,64]{2,1,0:T(4,128)S(1)} %slice.1227), channel_id=1, source_target_pairs={{4,0},{8,4},{12,8},{16,12},{20,16},{24,20},{28,24},{32,28},{36,32}... | collective-permute-start | bytes 3080 | tf_op jit(solution)/shard_map/ppermute | solution.py:23
  161.2 5.1 collective-permute-start.27
  173.1 8.3 %collective-permute-start.29 = (f32[1,4,64]{2,1,0:T(4,128)S(1)}, f32[1,4,64]{2,1,0:T(4,128)S(1)}, u32[]{:S(2)}, u32[]{:S(2)}) collective-permute-start(f32[1,4,64]{2,1,0:T(4,128)S(1)} %slice.1243), channel_id=1, source_target_pairs={{4,0},{8,4},{12,8},{16,12},{20,16},{24,20},{28,24},{32,28},{36,32}... | collective-permute-start | bytes 3080 | tf_op jit(solution)/shard_map/ppermute | solution.py:23
  182.3 3.3 collective-permute-start.30
  185.6 3.7 collective-permute-start.31
  191.3 4.6 collective-permute-start.39
  200.0 8.8 %collective-permute-start.33 = (f32[1,2,32]{2,1,0:T(2,128)S(1)}, f32[1,2,32]{2,1,0:T(2,128)S(1)}, u32[]{:S(2)}, u32[]{:S(2)}) collective-permute-start(f32[1,2,32]{2,1,0:T(2,128)S(1)} %slice.1259), channel_id=1, source_target_pairs={{4,0},{8,4},{12,8},{16,12},{20,16},{24,20},{28,24},{32,28},{36,32}... | collective-permute-start | bytes 776 | tf_op jit(solution)/shard_map/ppermute | solution.py:23
  211.0 4.6 collective-permute-start.35
  221.6 8.6 %collective-permute-start.41 = (f32[1,2,32]{2,1,0:T(2,128)S(1)}, f32[1,2,32]{2,1,0:T(2,128)S(1)}, u32[]{:S(2)}, u32[]{:S(2)}) collective-permute-start(f32[1,2,32]{2,1,0:T(2,128)S(1)} %slice.1291), channel_id=1, source_target_pairs={{4,0},{8,4},{12,8},{16,12},{20,16},{24,20},{28,24},{32,28},{36,32}... | collective-permute-start | bytes 776 | tf_op jit(solution)/shard_map/ppermute | solution.py:23
  232.9 5.1 collective-permute-start.43
  244.1 8.3 %collective-permute-start.45 = (f32[1,4,64]{2,1,0:T(4,128)S(1)}, f32[1,4,64]{2,1,0:T(4,128)S(1)}, u32[]{:S(2)}, u32[]{:S(2)}) collective-permute-start(f32[1,4,64]{2,1,0:T(4,128)S(1)} %slice.1307), channel_id=1, source_target_pairs={{4,0},{8,4},{12,8},{16,12},{20,16},{24,20},{28,24},{32,28},{36,32}... | collective-permute-start | bytes 3080 | tf_op jit(solution)/shard_map/ppermute | solution.py:23
  253.2 3.3 collective-permute-start.46
  256.5 3.7 collective-permute-start.47
  268.6 8.6 %collective-permute-start.49 = (f32[1,8,128]{2,1,0:T(8,128)S(1)}, f32[1,8,128]{2,1,0:T(8,128)S(1)}, u32[]{:S(2)}, u32[]{:S(2)}) collective-permute-start(f32[1,8,128]{2,1,0:T(8,128)S(1)} %slice.1324), channel_id=1, source_target_pairs={{4,0},{8,4},{12,8},{16,12},{20,16},{24,20},{28,24},{32,28},{36,32}... | collective-permute-start | bytes 12296 | tf_op jit(solution)/shard_map/ppermute | solution.py:23
  278.1 3.6 collective-permute-start.50
  281.7 3.1 collective-permute-start.51
  286.7 3.7 fusion.538
  296.5 8.9 %collective-permute-start.53 = (f32[1,8,128]{2,1,0:T(8,128)S(1)}, f32[1,8,128]{2,1,0:T(8,128)S(1)}, u32[]{:S(2)}, u32[]{:S(2)}) collective-permute-start(f32[1,8,128]{2,1,0:T(8,128)S(1)} %slice.1338), channel_id=1, source_target_pairs={{4,0},{8,4},{12,8},{16,12},{20,16},{24,20},{28,24},{32,28},{36,32}... | collective-permute-start | bytes 12296 | tf_op jit(solution)/shard_map/ppermute | solution.py:23
  309.2 3.6 collective-permute-start.55
  314.2 3.7 fusion.540
  324.0 8.9 %collective-permute-start.57 = (f32[1,8,128]{2,1,0:T(8,128)S(1)}, f32[1,8,128]{2,1,0:T(8,128)S(1)}, u32[]{:S(2)}, u32[]{:S(2)}) collective-permute-start(f32[1,8,128]{2,1,0:T(8,128)S(1)} %slice.1352), channel_id=1, source_target_pairs={{4,0},{8,4},{12,8},{16,12},{20,16},{24,20},{28,24},{32,28},{36,32}... | collective-permute-start | bytes 12296 | tf_op jit(solution)/shard_map/ppermute | solution.py:23
  336.6 4.1 collective-permute-start.59
  341.9 3.7 fusion.542
  351.7 8.6 %collective-permute-start.61 = (f32[1,8,128]{2,1,0:T(8,128)S(1)}, f32[1,8,128]{2,1,0:T(8,128)S(1)}, u32[]{:S(2)}, u32[]{:S(2)}) collective-permute-start(f32[1,8,128]{2,1,0:T(8,128)S(1)} %slice.1366), channel_id=1, source_target_pairs={{4,0},{8,4},{12,8},{16,12},{20,16},{24,20},{28,24},{32,28},{36,32}... | collective-permute-start | bytes 12296 | tf_op jit(solution)/shard_map/ppermute | solution.py:23
  364.2 3.7 collective-permute-start.63
  373.1 8.6 %collective-permute-start.65 = (f32[1,4,64]{2,1,0:T(4,128)S(1)}, f32[1,4,64]{2,1,0:T(4,128)S(1)}, u32[]{:S(2)}, u32[]{:S(2)}) collective-permute-start(f32[1,4,64]{2,1,0:T(4,128)S(1)} %slice.1379), channel_id=1, source_target_pairs={{4,0},{8,4},{12,8},{16,12},{20,16},{24,20},{28,24},{32,28},{36,32}... | collective-permute-start | bytes 3080 | tf_op jit(solution)/shard_map/ppermute | solution.py:23
  382.5 3.6 collective-permute-start.66
  396.6 8.9 %collective-permute-start.69 = (f32[1,4,64]{2,1,0:T(4,128)S(1)}, f32[1,4,64]{2,1,0:T(4,128)S(1)}, u32[]{:S(2)}, u32[]{:S(2)}) collective-permute-start(f32[1,4,64]{2,1,0:T(4,128)S(1)} %slice.1395), channel_id=1, source_target_pairs={{4,0},{8,4},{12,8},{16,12},{20,16},{24,20},{28,24},{32,28},{36,32}... | collective-permute-start | bytes 3080 | tf_op jit(solution)/shard_map/ppermute | solution.py:23
  409.1 3.6 collective-permute-start.71
  419.6 8.9 %collective-permute-start.73 = (f32[1,4,64]{2,1,0:T(4,128)S(1)}, f32[1,4,64]{2,1,0:T(4,128)S(1)}, u32[]{:S(2)}, u32[]{:S(2)}) collective-permute-start(f32[1,4,64]{2,1,0:T(4,128)S(1)} %slice.1411), channel_id=1, source_target_pairs={{4,0},{8,4},{12,8},{16,12},{20,16},{24,20},{28,24},{32,28},{36,32}... | collective-permute-start | bytes 3080 | tf_op jit(solution)/shard_map/ppermute | solution.py:23
  432.1 3.9 collective-permute-start.75
  440.3 8.6 %collective-permute-start.77 = (f32[1,2,32]{2,1,0:T(2,128)S(1)}, f32[1,2,32]{2,1,0:T(2,128)S(1)}, u32[]{:S(2)}, u32[]{:S(2)}) collective-permute-start(f32[1,2,32]{2,1,0:T(2,128)S(1)} %slice.1427), channel_id=1, source_target_pairs={{4,0},{8,4},{12,8},{16,12},{20,16},{24,20},{28,24},{32,28},{36,32}... | collective-permute-start | bytes 776 | tf_op jit(solution)/shard_map/ppermute | solution.py:23
  452.8 4.2 collective-permute-start.79
  461.9 8.6 %collective-permute-start.81 = (f32[1,2,32]{2,1,0:T(2,128)S(1)}, f32[1,2,32]{2,1,0:T(2,128)S(1)}, u32[]{:S(2)}, u32[]{:S(2)}) collective-permute-start(f32[1,2,32]{2,1,0:T(2,128)S(1)} %slice.1443), channel_id=1, source_target_pairs={{4,0},{8,4},{12,8},{16,12},{20,16},{24,20},{28,24},{32,28},{36,32}... | collective-permute-start | bytes 776 | tf_op jit(solution)/shard_map/ppermute | solution.py:23
  471.3 3.6 collective-permute-start.82
  484.7 8.9 %collective-permute-start.85 = (f32[1,4,64]{2,1,0:T(4,128)S(1)}, f32[1,4,64]{2,1,0:T(4,128)S(1)}, u32[]{:S(2)}, u32[]{:S(2)}) collective-permute-start(f32[1,4,64]{2,1,0:T(4,128)S(1)} %slice.1459), channel_id=1, source_target_pairs={{4,0},{8,4},{12,8},{16,12},{20,16},{24,20},{28,24},{32,28},{36,32}... | collective-permute-start | bytes 3080 | tf_op jit(solution)/shard_map/ppermute | solution.py:23
  497.2 3.6 collective-permute-start.87
  509.0 8.9 %collective-permute-start.89 = (f32[1,8,128]{2,1,0:T(8,128)S(1)}, f32[1,8,128]{2,1,0:T(8,128)S(1)}, u32[]{:S(2)}, u32[]{:S(2)}) collective-permute-start(f32[1,8,128]{2,1,0:T(8,128)S(1)} %slice.1476), channel_id=1, source_target_pairs={{4,0},{8,4},{12,8},{16,12},{20,16},{24,20},{28,24},{32,28},{36,32}... | collective-permute-start | bytes 12296 | tf_op jit(solution)/shard_map/ppermute | solution.py:23
  521.7 4.1 collective-permute-start.91
  526.9 3.7 fusion.551
  536.7 8.6 %collective-permute-start.93 = (f32[1,8,128]{2,1,0:T(8,128)S(1)}, f32[1,8,128]{2,1,0:T(8,128)S(1)}, u32[]{:S(2)}, u32[]{:S(2)}) collective-permute-start(f32[1,8,128]{2,1,0:T(8,128)S(1)} %slice.1490), channel_id=1, source_target_pairs={{4,0},{8,4},{12,8},{16,12},{20,16},{24,20},{28,24},{32,28},{36,32}... | collective-permute-start | bytes 12296 | tf_op jit(solution)/shard_map/ppermute | solution.py:23
  549.3 3.8 collective-permute-start.95
  554.8 6.6 %all-reduce.2 = (f32[]{:T(128)}, f32[]{:T(128)}, f32[]{:T(128)}) all-reduce(f32[]{:T(128)} %get-tuple-element.4, f32[]{:T(128)} %get-tuple-element.5, f32[]{:T(128)} %get-tuple-element.3), channel_id=1, replica_groups=mesh['gx_0'=4,'gx_1'=32,'gx_2'=2,'gy'=4] {'gx_0'}, use_global_device_ids=true, to_apply=%region_4.5 | all-reduce | flops 3 | bytes 24 | tf_op jit(solution)/shard_map/psum | solution.py:31
  561.5 50.1 %all-reduce = (f32[]{:T(128)}, f32[]{:T(128)}, f32[]{:T(128)}) all-reduce(f32[]{:T(128)} %get-tuple-element.12, f32[]{:T(128)} %get-tuple-element.13, f32[]{:T(128)} %get-tuple-element.14), channel_id=1, replica_groups=mesh['gx_0'=4,'gx_1'=32,'gx_2'=2,'gy'=4] {'gx_1'}, use_global_device_ids=true, to_apply=%region_5.6 | all-reduce | flops 3 | bytes 24 | tf_op jit(solution)/shard_map/psum | solution.py:31
  611.6 14.8 %all-reduce.3 = (f32[]{:T(128)}, f32[]{:T(128)}, f32[]{:T(128)}) all-reduce(f32[]{:T(128)} %get-tuple-element.6, f32[]{:T(128)} %get-tuple-element.7, f32[]{:T(128)} %get-tuple-element.8), channel_id=1, replica_groups=mesh['gx_0'=4,'gx_1'=32,'gx_2'=2,'gy'=4] {'gx_2'}, use_global_device_ids=true, to_apply=%region_6.7 | all-reduce | flops 3 | bytes 24 | tf_op jit(solution)/shard_map/psum | solution.py:31
  626.3 9.4 %all-reduce.1 = (f32[]{:T(128)}, f32[]{:T(128)}, f32[]{:T(128)}) all-reduce(f32[]{:T(128)} %get-tuple-element.15, f32[]{:T(128)} %get-tuple-element.16, f32[]{:T(128)} %get-tuple-element.17), channel_id=1, replica_groups=mesh['gx_0'=4,'gx_1'=32,'gx_2'=2,'gy'=4] {'gy'}, use_global_device_ids=true, to_apply=%region_7.8 | all-reduce | flops 3 | bytes 24 | tf_op jit(solution)/shard_map/psum | solution.py:31
  (776 shorter events, 209.6 us)
Async XLA Ops:
  1.3 33.9 %collective-permute-start = (f32[1,8,128]{2,1,0:T(8,128)S(1)}, f32[1,8,128]{2,1,0:T(8,128)S(1)}, u32[]{:S(2)}, u32[]{:S(2)}) collective-permute-start(f32[1,8,128]{2,1,0:T(8,128)S(1)} %get-tuple-element.140), channel_id=1, source_target_pairs={{0,4},{4,8},{8,12},{12,16},{16,20},{20,24},{24,28},{28,32},{32,36}... | collective-permute-start | bytes 12296 | tf_op jit(solution)/shard_map/ppermute | solution.py:21
  6.4 28.8 %collective-permute-start.1 = (f32[1,8,128]{2,1,0:T(8,128)S(1)}, f32[1,8,128]{2,1,0:T(8,128)S(1)}, u32[]{:S(2)}, u32[]{:S(2)}) collective-permute-start(f32[1,8,128]{2,1,0:T(8,128)S(1)} %get-tuple-element.141), channel_id=1, source_target_pairs={{4,0},{8,4},{12,8},{16,12},{20,16},{24,20},{28,24},{32,28},{36,32}... | collective-permute-start | bytes 12296 | tf_op jit(solution)/shard_map/ppermute | solution.py:23
  19.6 153.1 %collective-permute-start.37 = (f32[1,2,32]{2,1,0:T(2,128)S(1)}, f32[1,2,32]{2,1,0:T(2,128)S(1)}, u32[]{:S(2)}, u32[]{:S(2)}) collective-permute-start(f32[1,2,32]{2,1,0:T(2,128)S(1)} %slice.1273), channel_id=1, source_target_pairs={{4,0},{8,4},{12,8},{16,12},{20,16},{24,20},{28,24},{32,28},{36,32}... | collective-permute-start | bytes 776 | tf_op jit(solution)/shard_map/ppermute | solution.py:23
  28.2 14.6 %collective-permute-start.4 = (f32[1,8,128]{2,1,0:T(8,128)S(1)}, f32[1,8,128]{2,1,0:T(8,128)S(1)}, u32[]{:S(2)}, u32[]{:S(2)}) collective-permute-start(f32[1,8,128]{2,1,0:T(8,128)S(1)} %slice.1151), channel_id=1, source_target_pairs={{0,4},{4,8},{8,12},{12,16},{16,20},{20,24},{24,28},{28,32},{32,36}... | collective-permute-start | bytes 12296 | tf_op jit(solution)/shard_map/ppermute | solution.py:21
  30.3 16.0 %collective-permute-start.5 = (f32[1,8,128]{2,1,0:T(8,128)S(1)}, f32[1,8,128]{2,1,0:T(8,128)S(1)}, u32[]{:S(2)}, u32[]{:S(2)}) collective-permute-start(f32[1,8,128]{2,1,0:T(8,128)S(1)} %slice.1154), channel_id=1, source_target_pairs={{4,0},{8,4},{12,8},{16,12},{20,16},{24,20},{28,24},{32,28},{36,32}... | collective-permute-start | bytes 12296 | tf_op jit(solution)/shard_map/ppermute | solution.py:23
  36.1 12.2 %collective-permute-start.2 = (f32[8,1,128]{2,1,0:T(1,128)S(1)}, f32[8,1,128]{2,1,0:T(1,128)S(1)}, u32[]{:S(2)}, u32[]{:S(2)}) collective-permute-start(f32[8,1,128]{2,1,0:T(1,128)S(1)} %get-tuple-element.138), channel_id=1, source_target_pairs={{0,1},{1,2},{2,3},{3,0},{4,5},{5,6},{6,7},{7,4},{8,9},{9,10},{10,1... | collective-permute-start | bytes 12296 | tf_op jit(solution)/shard_map/ppermute | solution.py:21
  39.2 9.1 %collective-permute-start.3 = (f32[8,1,128]{2,1,0:T(1,128)S(1)}, f32[8,1,128]{2,1,0:T(1,128)S(1)}, u32[]{:S(2)}, u32[]{:S(2)}) collective-permute-start(f32[8,1,128]{2,1,0:T(1,128)S(1)} %get-tuple-element.139), channel_id=1, source_target_pairs={{1,0},{2,1},{3,2},{0,3},{5,4},{6,5},{7,6},{4,7},{9,8},{10,9},{11,1... | collective-permute-start | bytes 12296 | tf_op jit(solution)/shard_map/ppermute | solution.py:23
  42.8 130.0 %collective-permute-start.36 = (f32[1,2,32]{2,1,0:T(2,128)S(1)}, f32[1,2,32]{2,1,0:T(2,128)S(1)}, u32[]{:S(2)}, u32[]{:S(2)}) collective-permute-start(f32[1,2,32]{2,1,0:T(2,128)S(1)} %slice.1273), channel_id=1, source_target_pairs={{0,4},{4,8},{8,12},{12,16},{16,20},{20,24},{24,28},{28,32},{32,36}... | collective-permute-start | bytes 776 | tf_op jit(solution)/shard_map/ppermute | solution.py:21
  46.3 75.0 %collective-permute-start.20 = (f32[1,4,64]{2,1,0:T(4,128)S(1)}, f32[1,4,64]{2,1,0:T(4,128)S(1)}, u32[]{:S(2)}, u32[]{:S(2)}) collective-permute-start(f32[1,4,64]{2,1,0:T(4,128)S(1)} %slice.1209), channel_id=1, source_target_pairs={{0,4},{4,8},{8,12},{12,16},{16,20},{20,24},{24,28},{28,32},{32,36}... | collective-permute-start | bytes 3080 | tf_op jit(solution)/shard_map/ppermute | solution.py:21
  64.4 9.7 %collective-permute-start.8 = (f32[1,8,128]{2,1,0:T(8,128)S(1)}, f32[1,8,128]{2,1,0:T(8,128)S(1)}, u32[]{:S(2)}, u32[]{:S(2)}) collective-permute-start(f32[1,8,128]{2,1,0:T(8,128)S(1)} %slice.1165), channel_id=1, source_target_pairs={{0,4},{4,8},{8,12},{12,16},{16,20},{20,24},{24,28},{28,32},{32,36}... | collective-permute-start | bytes 12296 | tf_op jit(solution)/shard_map/ppermute | solution.py:21
  74.4 7.4 %collective-permute-start.10 = (f32[8,1,128]{2,1,0:T(1,128)S(1)}, f32[8,1,128]{2,1,0:T(1,128)S(1)}, u32[]{:S(2)}, u32[]{:S(2)}) collective-permute-start(f32[8,1,128]{2,1,0:T(1,128)S(1)} %get-tuple-element.132), channel_id=1, source_target_pairs={{0,1},{1,2},{2,3},{3,0},{4,5},{5,6},{6,7},{7,4},{8,9},{9,10},{10,1... | collective-permute-start | bytes 12296 | tf_op jit(solution)/shard_map/ppermute | solution.py:21
  90.5 11.0 %collective-permute-start.12 = (f32[1,8,128]{2,1,0:T(8,128)S(1)}, f32[1,8,128]{2,1,0:T(8,128)S(1)}, u32[]{:S(2)}, u32[]{:S(2)}) collective-permute-start(f32[1,8,128]{2,1,0:T(8,128)S(1)} %slice.1179), channel_id=1, source_target_pairs={{0,4},{4,8},{8,12},{12,16},{16,20},{20,24},{24,28},{28,32},{32,36}... | collective-permute-start | bytes 12296 | tf_op jit(solution)/shard_map/ppermute | solution.py:21
  92.6 9.1 %collective-permute-start.13 = (f32[1,8,128]{2,1,0:T(8,128)S(1)}, f32[1,8,128]{2,1,0:T(8,128)S(1)}, u32[]{:S(2)}, u32[]{:S(2)}) collective-permute-start(f32[1,8,128]{2,1,0:T(8,128)S(1)} %slice.1182), channel_id=1, source_target_pairs={{4,0},{8,4},{12,8},{16,12},{20,16},{24,20},{28,24},{32,28},{36,32}... | collective-permute-start | bytes 12296 | tf_op jit(solution)/shard_map/ppermute | solution.py:23
  101.9 7.4 %collective-permute-start.14 = (f32[8,1,128]{2,1,0:T(1,128)S(1)}, f32[8,1,128]{2,1,0:T(1,128)S(1)}, u32[]{:S(2)}, u32[]{:S(2)}) collective-permute-start(f32[8,1,128]{2,1,0:T(1,128)S(1)} %get-tuple-element.126), channel_id=1, source_target_pairs={{0,1},{1,2},{2,3},{3,0},{4,5},{5,6},{6,7},{7,4},{8,9},{9,10},{10,1... | collective-permute-start | bytes 12296 | tf_op jit(solution)/shard_map/ppermute | solution.py:21
  105.2 11.8 %collective-permute-start.15 = (f32[8,1,128]{2,1,0:T(1,128)S(1)}, f32[8,1,128]{2,1,0:T(1,128)S(1)}, u32[]{:S(2)}, u32[]{:S(2)}) collective-permute-start(f32[8,1,128]{2,1,0:T(1,128)S(1)} %get-tuple-element.127), channel_id=1, source_target_pairs={{1,0},{2,1},{3,2},{0,3},{5,4},{6,5},{7,6},{4,7},{9,8},{10,9},{11,1... | collective-permute-start | bytes 12296 | tf_op jit(solution)/shard_map/ppermute | solution.py:23
  109.2 12.1 %collective-permute-start.21 = (f32[1,4,64]{2,1,0:T(4,128)S(1)}, f32[1,4,64]{2,1,0:T(4,128)S(1)}, u32[]{:S(2)}, u32[]{:S(2)}) collective-permute-start(f32[1,4,64]{2,1,0:T(4,128)S(1)} %slice.1211), channel_id=1, source_target_pairs={{4,0},{8,4},{12,8},{16,12},{20,16},{24,20},{28,24},{32,28},{36,32}... | collective-permute-start | bytes 3080 | tf_op jit(solution)/shard_map/ppermute | solution.py:23
  119.4 9.0 %collective-permute-start.16 = (f32[1,4,64]{2,1,0:T(4,128)S(1)}, f32[1,4,64]{2,1,0:T(4,128)S(1)}, u32[]{:S(2)}, u32[]{:S(2)}) collective-permute-start(f32[1,4,64]{2,1,0:T(4,128)S(1)} %slice.1193), channel_id=1, source_target_pairs={{0,4},{4,8},{8,12},{12,16},{16,20},{20,24},{24,28},{28,32},{32,36}... | collective-permute-start | bytes 3080 | tf_op jit(solution)/shard_map/ppermute | solution.py:21
  121.4 17.0 %collective-permute-start.22 = (f32[6,1,64]{2,1,0:T(1,128)S(1)}, f32[6,1,64]{2,1,0:T(1,128)S(1)}, u32[]{:S(2)}, u32[]{:S(2)}) collective-permute-start(f32[6,1,64]{2,1,0:T(1,128)S(1)} %get-tuple-element.164), channel_id=1, source_target_pairs={{0,1},{1,2},{2,3},{3,0},{4,5},{5,6},{6,7},{7,4},{8,9},{9,10},{10,1... | collective-permute-start | bytes 4616 | tf_op jit(solution)/shard_map/ppermute | solution.py:21
  123.3 19.6 %collective-permute-start.23 = (f32[6,1,64]{2,1,0:T(1,128)S(1)}, f32[6,1,64]{2,1,0:T(1,128)S(1)}, u32[]{:S(2)}, u32[]{:S(2)}) collective-permute-start(f32[6,1,64]{2,1,0:T(1,128)S(1)} %get-tuple-element.165), channel_id=1, source_target_pairs={{1,0},{2,1},{3,2},{0,3},{5,4},{6,5},{7,6},{4,7},{9,8},{10,9},{11,1... | collective-permute-start | bytes 4616 | tf_op jit(solution)/shard_map/ppermute | solution.py:23
  128.4 8.0 %collective-permute-start.17 = (f32[1,4,64]{2,1,0:T(4,128)S(1)}, f32[1,4,64]{2,1,0:T(4,128)S(1)}, u32[]{:S(2)}, u32[]{:S(2)}) collective-permute-start(f32[1,4,64]{2,1,0:T(4,128)S(1)} %slice.1195), channel_id=1, source_target_pairs={{4,0},{8,4},{12,8},{16,12},{20,16},{24,20},{28,24},{32,28},{36,32}... | collective-permute-start | bytes 3080 | tf_op jit(solution)/shard_map/ppermute | solution.py:23
  148.1 10.4 %collective-permute-start.24 = (f32[1,4,64]{2,1,0:T(4,128)S(1)}, f32[1,4,64]{2,1,0:T(4,128)S(1)}, u32[]{:S(2)}, u32[]{:S(2)}) collective-permute-start(f32[1,4,64]{2,1,0:T(4,128)S(1)} %slice.1225), channel_id=1, source_target_pairs={{0,4},{4,8},{8,12},{12,16},{16,20},{20,24},{24,28},{28,32},{32,36}... | collective-permute-start | bytes 3080 | tf_op jit(solution)/shard_map/ppermute | solution.py:21
  150.4 8.8 %collective-permute-start.25 = (f32[1,4,64]{2,1,0:T(4,128)S(1)}, f32[1,4,64]{2,1,0:T(4,128)S(1)}, u32[]{:S(2)}, u32[]{:S(2)}) collective-permute-start(f32[1,4,64]{2,1,0:T(4,128)S(1)} %slice.1227), channel_id=1, source_target_pairs={{4,0},{8,4},{12,8},{16,12},{20,16},{24,20},{28,24},{32,28},{36,32}... | collective-permute-start | bytes 3080 | tf_op jit(solution)/shard_map/ppermute | solution.py:23
  159.3 7.3 %collective-permute-start.26 = (f32[6,1,64]{2,1,0:T(1,128)S(1)}, f32[6,1,64]{2,1,0:T(1,128)S(1)}, u32[]{:S(2)}, u32[]{:S(2)}) collective-permute-start(f32[6,1,64]{2,1,0:T(1,128)S(1)} %get-tuple-element.160), channel_id=1, source_target_pairs={{0,1},{1,2},{2,3},{3,0},{4,5},{5,6},{6,7},{7,4},{8,9},{9,10},{10,1... | collective-permute-start | bytes 4616 | tf_op jit(solution)/shard_map/ppermute | solution.py:21
  170.8 10.8 %collective-permute-start.28 = (f32[1,4,64]{2,1,0:T(4,128)S(1)}, f32[1,4,64]{2,1,0:T(4,128)S(1)}, u32[]{:S(2)}, u32[]{:S(2)}) collective-permute-start(f32[1,4,64]{2,1,0:T(4,128)S(1)} %slice.1241), channel_id=1, source_target_pairs={{0,4},{4,8},{8,12},{12,16},{16,20},{20,24},{24,28},{28,32},{32,36}... | collective-permute-start | bytes 3080 | tf_op jit(solution)/shard_map/ppermute | solution.py:21
  173.1 9.1 %collective-permute-start.29 = (f32[1,4,64]{2,1,0:T(4,128)S(1)}, f32[1,4,64]{2,1,0:T(4,128)S(1)}, u32[]{:S(2)}, u32[]{:S(2)}) collective-permute-start(f32[1,4,64]{2,1,0:T(4,128)S(1)} %slice.1243), channel_id=1, source_target_pairs={{4,0},{8,4},{12,8},{16,12},{20,16},{24,20},{28,24},{32,28},{36,32}... | collective-permute-start | bytes 3080 | tf_op jit(solution)/shard_map/ppermute | solution.py:23
  182.3 13.6 %collective-permute-start.30 = (f32[6,1,64]{2,1,0:T(1,128)S(1)}, f32[6,1,64]{2,1,0:T(1,128)S(1)}, u32[]{:S(2)}, u32[]{:S(2)}) collective-permute-start(f32[6,1,64]{2,1,0:T(1,128)S(1)} %get-tuple-element.158), channel_id=1, source_target_pairs={{0,1},{1,2},{2,3},{3,0},{4,5},{5,6},{6,7},{7,4},{8,9},{9,10},{10,1... | collective-permute-start | bytes 4616 | tf_op jit(solution)/shard_map/ppermute | solution.py:21
  185.6 10.3 %collective-permute-start.31 = (f32[6,1,64]{2,1,0:T(1,128)S(1)}, f32[6,1,64]{2,1,0:T(1,128)S(1)}, u32[]{:S(2)}, u32[]{:S(2)}) collective-permute-start(f32[6,1,64]{2,1,0:T(1,128)S(1)} %get-tuple-element.159), channel_id=1, source_target_pairs={{1,0},{2,1},{3,2},{0,3},{5,4},{6,5},{7,6},{4,7},{9,8},{10,9},{11,1... | collective-permute-start | bytes 4616 | tf_op jit(solution)/shard_map/ppermute | solution.py:23
  189.3 26.3 %collective-permute-start.38 = (f32[4,1,32]{2,1,0:T(1,128)S(1)}, f32[4,1,32]{2,1,0:T(1,128)S(1)}, u32[]{:S(2)}, u32[]{:S(2)}) collective-permute-start(f32[4,1,32]{2,1,0:T(1,128)S(1)} %get-tuple-element.216), channel_id=1, source_target_pairs={{0,1},{1,2},{2,3},{3,0},{4,5},{5,6},{6,7},{7,4},{8,9},{9,10},{10,1... | collective-permute-start | bytes 1544 | tf_op jit(solution)/shard_map/ppermute | solution.py:21
  191.3 24.4 %collective-permute-start.39 = (f32[4,1,32]{2,1,0:T(1,128)S(1)}, f32[4,1,32]{2,1,0:T(1,128)S(1)}, u32[]{:S(2)}, u32[]{:S(2)}) collective-permute-start(f32[4,1,32]{2,1,0:T(1,128)S(1)} %get-tuple-element.217), channel_id=1, source_target_pairs={{1,0},{2,1},{3,2},{0,3},{5,4},{6,5},{7,6},{4,7},{9,8},{10,9},{11,1... | collective-permute-start | bytes 1544 | tf_op jit(solution)/shard_map/ppermute | solution.py:23
  197.9 11.0 %collective-permute-start.32 = (f32[1,2,32]{2,1,0:T(2,128)S(1)}, f32[1,2,32]{2,1,0:T(2,128)S(1)}, u32[]{:S(2)}, u32[]{:S(2)}) collective-permute-start(f32[1,2,32]{2,1,0:T(2,128)S(1)} %slice.1257), channel_id=1, source_target_pairs={{0,4},{4,8},{8,12},{12,16},{16,20},{20,24},{24,28},{28,32},{32,36}... | collective-permute-start | bytes 776 | tf_op jit(solution)/shard_map/ppermute | solution.py:21
  200.0 9.1 %collective-permute-start.33 = (f32[1,2,32]{2,1,0:T(2,128)S(1)}, f32[1,2,32]{2,1,0:T(2,128)S(1)}, u32[]{:S(2)}, u32[]{:S(2)}) collective-permute-start(f32[1,2,32]{2,1,0:T(2,128)S(1)} %slice.1259), channel_id=1, source_target_pairs={{4,0},{8,4},{12,8},{16,12},{20,16},{24,20},{28,24},{32,28},{36,32}... | collective-permute-start | bytes 776 | tf_op jit(solution)/shard_map/ppermute | solution.py:23
  219.5 10.8 %collective-permute-start.40 = (f32[1,2,32]{2,1,0:T(2,128)S(1)}, f32[1,2,32]{2,1,0:T(2,128)S(1)}, u32[]{:S(2)}, u32[]{:S(2)}) collective-permute-start(f32[1,2,32]{2,1,0:T(2,128)S(1)} %slice.1289), channel_id=1, source_target_pairs={{0,4},{4,8},{8,12},{12,16},{16,20},{20,24},{24,28},{28,32},{32,36}... | collective-permute-start | bytes 776 | tf_op jit(solution)/shard_map/ppermute | solution.py:21
  221.6 9.4 %collective-permute-start.41 = (f32[1,2,32]{2,1,0:T(2,128)S(1)}, f32[1,2,32]{2,1,0:T(2,128)S(1)}, u32[]{:S(2)}, u32[]{:S(2)}) collective-permute-start(f32[1,2,32]{2,1,0:T(2,128)S(1)} %slice.1291), channel_id=1, source_target_pairs={{4,0},{8,4},{12,8},{16,12},{20,16},{24,20},{28,24},{32,28},{36,32}... | collective-permute-start | bytes 776 | tf_op jit(solution)/shard_map/ppermute | solution.py:23
  231.0 7.0 %collective-permute-start.42 = (f32[4,1,32]{2,1,0:T(1,128)S(1)}, f32[4,1,32]{2,1,0:T(1,128)S(1)}, u32[]{:S(2)}, u32[]{:S(2)}) collective-permute-start(f32[4,1,32]{2,1,0:T(1,128)S(1)} %get-tuple-element.212), channel_id=1, source_target_pairs={{0,1},{1,2},{2,3},{3,0},{4,5},{5,6},{6,7},{7,4},{8,9},{9,10},{10,1... | collective-permute-start | bytes 1544 | tf_op jit(solution)/shard_map/ppermute | solution.py:21
  241.8 10.7 %collective-permute-start.44 = (f32[1,4,64]{2,1,0:T(4,128)S(1)}, f32[1,4,64]{2,1,0:T(4,128)S(1)}, u32[]{:S(2)}, u32[]{:S(2)}) collective-permute-start(f32[1,4,64]{2,1,0:T(4,128)S(1)} %slice.1305), channel_id=1, source_target_pairs={{0,4},{4,8},{8,12},{12,16},{16,20},{20,24},{24,28},{28,32},{32,36}... | collective-permute-start | bytes 3080 | tf_op jit(solution)/shard_map/ppermute | solution.py:21
  244.1 9.1 %collective-permute-start.45 = (f32[1,4,64]{2,1,0:T(4,128)S(1)}, f32[1,4,64]{2,1,0:T(4,128)S(1)}, u32[]{:S(2)}, u32[]{:S(2)}) collective-permute-start(f32[1,4,64]{2,1,0:T(4,128)S(1)} %slice.1307), channel_id=1, source_target_pairs={{4,0},{8,4},{12,8},{16,12},{20,16},{24,20},{28,24},{32,28},{36,32}... | collective-permute-start | bytes 3080 | tf_op jit(solution)/shard_map/ppermute | solution.py:23
  253.2 7.3 %collective-permute-start.46 = (f32[6,1,64]{2,1,0:T(1,128)S(1)}, f32[6,1,64]{2,1,0:T(1,128)S(1)}, u32[]{:S(2)}, u32[]{:S(2)}) collective-permute-start(f32[6,1,64]{2,1,0:T(1,128)S(1)} %get-tuple-element.156), channel_id=1, source_target_pairs={{0,1},{1,2},{2,3},{3,0},{4,5},{5,6},{6,7},{7,4},{8,9},{9,10},{10,1... | collective-permute-start | bytes 4616 | tf_op jit(solution)/shard_map/ppermute | solution.py:21
  266.5 11.2 %collective-permute-start.48 = (f32[1,8,128]{2,1,0:T(8,128)S(1)}, f32[1,8,128]{2,1,0:T(8,128)S(1)}, u32[]{:S(2)}, u32[]{:S(2)}) collective-permute-start(f32[1,8,128]{2,1,0:T(8,128)S(1)} %slice.1321), channel_id=1, source_target_pairs={{0,4},{4,8},{8,12},{12,16},{16,20},{20,24},{24,28},{28,32},{32,36}... | collective-permute-start | bytes 12296 | tf_op jit(solution)/shard_map/ppermute | solution.py:21
  268.6 9.4 %collective-permute-start.49 = (f32[1,8,128]{2,1,0:T(8,128)S(1)}, f32[1,8,128]{2,1,0:T(8,128)S(1)}, u32[]{:S(2)}, u32[]{:S(2)}) collective-permute-start(f32[1,8,128]{2,1,0:T(8,128)S(1)} %slice.1324), channel_id=1, source_target_pairs={{4,0},{8,4},{12,8},{16,12},{20,16},{24,20},{28,24},{32,28},{36,32}... | collective-permute-start | bytes 12296 | tf_op jit(solution)/shard_map/ppermute | solution.py:23
  278.1 7.3 %collective-permute-start.50 = (f32[8,1,128]{2,1,0:T(1,128)S(1)}, f32[8,1,128]{2,1,0:T(1,128)S(1)}, u32[]{:S(2)}, u32[]{:S(2)}) collective-permute-start(f32[8,1,128]{2,1,0:T(1,128)S(1)} %get-tuple-element.110), channel_id=1, source_target_pairs={{0,1},{1,2},{2,3},{3,0},{4,5},{5,6},{6,7},{7,4},{8,9},{9,10},{10,1... | collective-permute-start | bytes 12296 | tf_op jit(solution)/shard_map/ppermute | solution.py:21
  294.4 11.5 %collective-permute-start.52 = (f32[1,8,128]{2,1,0:T(8,128)S(1)}, f32[1,8,128]{2,1,0:T(8,128)S(1)}, u32[]{:S(2)}, u32[]{:S(2)}) collective-permute-start(f32[1,8,128]{2,1,0:T(8,128)S(1)} %slice.1335), channel_id=1, source_target_pairs={{0,4},{4,8},{8,12},{12,16},{16,20},{20,24},{24,28},{28,32},{32,36}... | collective-permute-start | bytes 12296 | tf_op jit(solution)/shard_map/ppermute | solution.py:21
  296.5 9.7 %collective-permute-start.53 = (f32[1,8,128]{2,1,0:T(8,128)S(1)}, f32[1,8,128]{2,1,0:T(8,128)S(1)}, u32[]{:S(2)}, u32[]{:S(2)}) collective-permute-start(f32[1,8,128]{2,1,0:T(8,128)S(1)} %slice.1338), channel_id=1, source_target_pairs={{4,0},{8,4},{12,8},{16,12},{20,16},{24,20},{28,24},{32,28},{36,32}... | collective-permute-start | bytes 12296 | tf_op jit(solution)/shard_map/ppermute | solution.py:23
  321.8 11.5 %collective-permute-start.56 = (f32[1,8,128]{2,1,0:T(8,128)S(1)}, f32[1,8,128]{2,1,0:T(8,128)S(1)}, u32[]{:S(2)}, u32[]{:S(2)}) collective-permute-start(f32[1,8,128]{2,1,0:T(8,128)S(1)} %slice.1349), channel_id=1, source_target_pairs={{0,4},{4,8},{8,12},{12,16},{16,20},{20,24},{24,28},{28,32},{32,36}... | collective-permute-start | bytes 12296 | tf_op jit(solution)/shard_map/ppermute | solution.py:21
  324.0 9.7 %collective-permute-start.57 = (f32[1,8,128]{2,1,0:T(8,128)S(1)}, f32[1,8,128]{2,1,0:T(8,128)S(1)}, u32[]{:S(2)}, u32[]{:S(2)}) collective-permute-start(f32[1,8,128]{2,1,0:T(8,128)S(1)} %slice.1352), channel_id=1, source_target_pairs={{4,0},{8,4},{12,8},{16,12},{20,16},{24,20},{28,24},{32,28},{36,32}... | collective-permute-start | bytes 12296 | tf_op jit(solution)/shard_map/ppermute | solution.py:23
  349.6 11.2 %collective-permute-start.60 = (f32[1,8,128]{2,1,0:T(8,128)S(1)}, f32[1,8,128]{2,1,0:T(8,128)S(1)}, u32[]{:S(2)}, u32[]{:S(2)}) collective-permute-start(f32[1,8,128]{2,1,0:T(8,128)S(1)} %slice.1363), channel_id=1, source_target_pairs={{0,4},{4,8},{8,12},{12,16},{16,20},{20,24},{24,28},{28,32},{32,36}... | collective-permute-start | bytes 12296 | tf_op jit(solution)/shard_map/ppermute | solution.py:21
  351.7 9.4 %collective-permute-start.61 = (f32[1,8,128]{2,1,0:T(8,128)S(1)}, f32[1,8,128]{2,1,0:T(8,128)S(1)}, u32[]{:S(2)}, u32[]{:S(2)}) collective-permute-start(f32[1,8,128]{2,1,0:T(8,128)S(1)} %slice.1366), channel_id=1, source_target_pairs={{4,0},{8,4},{12,8},{16,12},{20,16},{24,20},{28,24},{32,28},{36,32}... | collective-permute-start | bytes 12296 | tf_op jit(solution)/shard_map/ppermute | solution.py:23
  370.8 11.0 %collective-permute-start.64 = (f32[1,4,64]{2,1,0:T(4,128)S(1)}, f32[1,4,64]{2,1,0:T(4,128)S(1)}, u32[]{:S(2)}, u32[]{:S(2)}) collective-permute-start(f32[1,4,64]{2,1,0:T(4,128)S(1)} %slice.1377), channel_id=1, source_target_pairs={{0,4},{4,8},{8,12},{12,16},{16,20},{20,24},{24,28},{28,32},{32,36}... | collective-permute-start | bytes 3080 | tf_op jit(solution)/shard_map/ppermute | solution.py:21
  373.1 9.4 %collective-permute-start.65 = (f32[1,4,64]{2,1,0:T(4,128)S(1)}, f32[1,4,64]{2,1,0:T(4,128)S(1)}, u32[]{:S(2)}, u32[]{:S(2)}) collective-permute-start(f32[1,4,64]{2,1,0:T(4,128)S(1)} %slice.1379), channel_id=1, source_target_pairs={{4,0},{8,4},{12,8},{16,12},{20,16},{24,20},{28,24},{32,28},{36,32}... | collective-permute-start | bytes 3080 | tf_op jit(solution)/shard_map/ppermute | solution.py:23
  394.3 11.3 %collective-permute-start.68 = (f32[1,4,64]{2,1,0:T(4,128)S(1)}, f32[1,4,64]{2,1,0:T(4,128)S(1)}, u32[]{:S(2)}, u32[]{:S(2)}) collective-permute-start(f32[1,4,64]{2,1,0:T(4,128)S(1)} %slice.1393), channel_id=1, source_target_pairs={{0,4},{4,8},{8,12},{12,16},{16,20},{20,24},{24,28},{28,32},{32,36}... | collective-permute-start | bytes 3080 | tf_op jit(solution)/shard_map/ppermute | solution.py:21
  396.6 9.7 %collective-permute-start.69 = (f32[1,4,64]{2,1,0:T(4,128)S(1)}, f32[1,4,64]{2,1,0:T(4,128)S(1)}, u32[]{:S(2)}, u32[]{:S(2)}) collective-permute-start(f32[1,4,64]{2,1,0:T(4,128)S(1)} %slice.1395), channel_id=1, source_target_pairs={{4,0},{8,4},{12,8},{16,12},{20,16},{24,20},{28,24},{32,28},{36,32}... | collective-permute-start | bytes 3080 | tf_op jit(solution)/shard_map/ppermute | solution.py:23
  417.3 11.3 %collective-permute-start.72 = (f32[1,4,64]{2,1,0:T(4,128)S(1)}, f32[1,4,64]{2,1,0:T(4,128)S(1)}, u32[]{:S(2)}, u32[]{:S(2)}) collective-permute-start(f32[1,4,64]{2,1,0:T(4,128)S(1)} %slice.1409), channel_id=1, source_target_pairs={{0,4},{4,8},{8,12},{12,16},{16,20},{20,24},{24,28},{28,32},{32,36}... | collective-permute-start | bytes 3080 | tf_op jit(solution)/shard_map/ppermute | solution.py:21
  419.6 9.7 %collective-permute-start.73 = (f32[1,4,64]{2,1,0:T(4,128)S(1)}, f32[1,4,64]{2,1,0:T(4,128)S(1)}, u32[]{:S(2)}, u32[]{:S(2)}) collective-permute-start(f32[1,4,64]{2,1,0:T(4,128)S(1)} %slice.1411), channel_id=1, source_target_pairs={{4,0},{8,4},{12,8},{16,12},{20,16},{24,20},{28,24},{32,28},{36,32}... | collective-permute-start | bytes 3080 | tf_op jit(solution)/shard_map/ppermute | solution.py:23
  438.2 10.8 %collective-permute-start.76 = (f32[1,2,32]{2,1,0:T(2,128)S(1)}, f32[1,2,32]{2,1,0:T(2,128)S(1)}, u32[]{:S(2)}, u32[]{:S(2)}) collective-permute-start(f32[1,2,32]{2,1,0:T(2,128)S(1)} %slice.1425), channel_id=1, source_target_pairs={{0,4},{4,8},{8,12},{12,16},{16,20},{20,24},{24,28},{28,32},{32,36}... | collective-permute-start | bytes 776 | tf_op jit(solution)/shard_map/ppermute | solution.py:21
  440.3 9.4 %collective-permute-start.77 = (f32[1,2,32]{2,1,0:T(2,128)S(1)}, f32[1,2,32]{2,1,0:T(2,128)S(1)}, u32[]{:S(2)}, u32[]{:S(2)}) collective-permute-start(f32[1,2,32]{2,1,0:T(2,128)S(1)} %slice.1427), channel_id=1, source_target_pairs={{4,0},{8,4},{12,8},{16,12},{20,16},{24,20},{28,24},{32,28},{36,32}... | collective-permute-start | bytes 776 | tf_op jit(solution)/shard_map/ppermute | solution.py:23
  449.7 7.2 %collective-permute-start.78 = (f32[4,1,32]{2,1,0:T(1,128)S(1)}, f32[4,1,32]{2,1,0:T(1,128)S(1)}, u32[]{:S(2)}, u32[]{:S(2)}) collective-permute-start(f32[4,1,32]{2,1,0:T(1,128)S(1)} %get-tuple-element.208), channel_id=1, source_target_pairs={{0,1},{1,2},{2,3},{3,0},{4,5},{5,6},{6,7},{7,4},{8,9},{9,10},{10,1... | collective-permute-start | bytes 1544 | tf_op jit(solution)/shard_map/ppermute | solution.py:21
  459.8 10.8 %collective-permute-start.80 = (f32[1,2,32]{2,1,0:T(2,128)S(1)}, f32[1,2,32]{2,1,0:T(2,128)S(1)}, u32[]{:S(2)}, u32[]{:S(2)}) collective-permute-start(f32[1,2,32]{2,1,0:T(2,128)S(1)} %slice.1441), channel_id=1, source_target_pairs={{0,4},{4,8},{8,12},{12,16},{16,20},{20,24},{24,28},{28,32},{32,36}... | collective-permute-start | bytes 776 | tf_op jit(solution)/shard_map/ppermute | solution.py:21
  461.9 9.4 %collective-permute-start.81 = (f32[1,2,32]{2,1,0:T(2,128)S(1)}, f32[1,2,32]{2,1,0:T(2,128)S(1)}, u32[]{:S(2)}, u32[]{:S(2)}) collective-permute-start(f32[1,2,32]{2,1,0:T(2,128)S(1)} %slice.1443), channel_id=1, source_target_pairs={{4,0},{8,4},{12,8},{16,12},{20,16},{24,20},{28,24},{32,28},{36,32}... | collective-permute-start | bytes 776 | tf_op jit(solution)/shard_map/ppermute | solution.py:23
  482.4 11.3 %collective-permute-start.84 = (f32[1,4,64]{2,1,0:T(4,128)S(1)}, f32[1,4,64]{2,1,0:T(4,128)S(1)}, u32[]{:S(2)}, u32[]{:S(2)}) collective-permute-start(f32[1,4,64]{2,1,0:T(4,128)S(1)} %slice.1457), channel_id=1, source_target_pairs={{0,4},{4,8},{8,12},{12,16},{16,20},{20,24},{24,28},{28,32},{32,36}... | collective-permute-start | bytes 3080 | tf_op jit(solution)/shard_map/ppermute | solution.py:21
  484.7 9.7 %collective-permute-start.85 = (f32[1,4,64]{2,1,0:T(4,128)S(1)}, f32[1,4,64]{2,1,0:T(4,128)S(1)}, u32[]{:S(2)}, u32[]{:S(2)}) collective-permute-start(f32[1,4,64]{2,1,0:T(4,128)S(1)} %slice.1459), channel_id=1, source_target_pairs={{4,0},{8,4},{12,8},{16,12},{20,16},{24,20},{28,24},{32,28},{36,32}... | collective-permute-start | bytes 3080 | tf_op jit(solution)/shard_map/ppermute | solution.py:23
  506.9 11.5 %collective-permute-start.88 = (f32[1,8,128]{2,1,0:T(8,128)S(1)}, f32[1,8,128]{2,1,0:T(8,128)S(1)}, u32[]{:S(2)}, u32[]{:S(2)}) collective-permute-start(f32[1,8,128]{2,1,0:T(8,128)S(1)} %slice.1473), channel_id=1, source_target_pairs={{0,4},{4,8},{8,12},{12,16},{16,20},{20,24},{24,28},{28,32},{32,36}... | collective-permute-start | bytes 12296 | tf_op jit(solution)/shard_map/ppermute | solution.py:21
  509.0 9.7 %collective-permute-start.89 = (f32[1,8,128]{2,1,0:T(8,128)S(1)}, f32[1,8,128]{2,1,0:T(8,128)S(1)}, u32[]{:S(2)}, u32[]{:S(2)}) collective-permute-start(f32[1,8,128]{2,1,0:T(8,128)S(1)} %slice.1476), channel_id=1, source_target_pairs={{4,0},{8,4},{12,8},{16,12},{20,16},{24,20},{28,24},{32,28},{36,32}... | collective-permute-start | bytes 12296 | tf_op jit(solution)/shard_map/ppermute | solution.py:23
  518.8 7.4 %collective-permute-start.90 = (f32[8,1,128]{2,1,0:T(1,128)S(1)}, f32[8,1,128]{2,1,0:T(1,128)S(1)}, u32[]{:S(2)}, u32[]{:S(2)}) collective-permute-start(f32[8,1,128]{2,1,0:T(1,128)S(1)} %get-tuple-element.78), channel_id=1, source_target_pairs={{0,1},{1,2},{2,3},{3,0},{4,5},{5,6},{6,7},{7,4},{8,9},{9,10},{10,1... | collective-permute-start | bytes 12296 | tf_op jit(solution)/shard_map/ppermute | solution.py:21
  534.6 11.2 %collective-permute-start.92 = (f32[1,8,128]{2,1,0:T(8,128)S(1)}, f32[1,8,128]{2,1,0:T(8,128)S(1)}, u32[]{:S(2)}, u32[]{:S(2)}) collective-permute-start(f32[1,8,128]{2,1,0:T(8,128)S(1)} %slice.1487), channel_id=1, source_target_pairs={{0,4},{4,8},{8,12},{12,16},{16,20},{20,24},{24,28},{28,32},{32,36}... | collective-permute-start | bytes 12296 | tf_op jit(solution)/shard_map/ppermute | solution.py:21
  536.7 9.4 %collective-permute-start.93 = (f32[1,8,128]{2,1,0:T(8,128)S(1)}, f32[1,8,128]{2,1,0:T(8,128)S(1)}, u32[]{:S(2)}, u32[]{:S(2)}) collective-permute-start(f32[1,8,128]{2,1,0:T(8,128)S(1)} %slice.1490), channel_id=1, source_target_pairs={{4,0},{8,4},{12,8},{16,12},{20,16},{24,20},{28,24},{32,28},{36,32}... | collective-permute-start | bytes 12296 | tf_op jit(solution)/shard_map/ppermute | solution.py:23
  (44 other events, 240.1 us)
where the time goes:
time: 653 us; the launch traced here: 643 us
  starting transfers between devices  414 us (63%)
  blocking collectives  80.8 us (12%)
  matrix products  62.1 us (10%)
  local copies, waits for them, and re-layouts  41 us (6%)
  waiting for transfers between devices  22.7 us (3%)
  other arithmetic  12.4 us (2%)
  between operations  10.1 us (2%)
    ppermute x48, starting transfers between devices, with_halo(): lax.ppermute(head, axis, [((i + 1) % count, i) for i in range(count)])  296 us
    ppermute x48, starting transfers between devices, with_halo(): lax.ppermute(tail, axis, [(i, (i + 1) % count) for i in range(count)])  118 us
    psum x4, blocking collectives, one_axis_at_a_time(): return functools.reduce(lax.psum, axes, shard)  80.8 us
    dot_general x16, matrix products, element_apply(): third = jnp.einsum('ak,eifjgk->eifjga', deriv, block, precision=high)  28.2 us
    ppermute x48, waiting for transfers between devices, with_halo(): lax.ppermute(head, axis, [((i + 1) % count, i) for i in range(count)])  22.6 us
  transfers between devices with their start and end apart: 96, of which 39 were waited for; matrix products, arithmetic and copies ran while one was open for 7% of the time, Pallas kernels for 0%

commit v1 on v0

v1 whole, which is shorter than its diff:
```python
import jax
import jax.numpy as jnp
import numpy as np
from jax import lax
from jax.experimental import pallas as pl
from jax.experimental.pallas import tpu as pltpu
from jax.sharding import PartitionSpec as P


def legendre_table(points, order):
    columns = [points * 0.0 + 1.0, points]
    for degree in range(2, order + 1):
        columns.append(((2 * degree - 1) * points * columns[-1] - (degree - 1) * columns[-2]) / degree)
    return np.stack(columns, axis=1)

def lobatto(count):
    order = count - 1
    points = np.cos(np.pi * np.arange(count) / order)
    for sweep in range(60):
        table = legendre_table(points, order)
        points = points - (points * table[:, order] - table[:, order - 1]) / (count * table[:, order])
    table = legendre_table(points, order)
    weights = 2.0 / (order * count * table[:, order] ** 2)
    values = table[:, order]
    points, weights, values = (points[::-1], weights[::-1], values[::-1])
    spread = points[:, None] - points[None, :] + np.eye(count)
    deriv = values[:, None] / values[None, :] / spread * (1.0 - np.eye(count))
    corner = order * (order + 1) / 4.0
    ends = np.array([-corner] + [0.0] * (count - 2) + [corner])
    return (points, weights, deriv + np.eye(count) * ends[None, :])

def lagrange(fine_points, coarse_points):
    columns = []
    for column in range(len(coarse_points)):
        value = fine_points * 0.0 + 1.0
        for other in range(len(coarse_points)):
            if other != column:
                value = value * (fine_points - coarse_points[other]) / (coarse_points[column] - coarse_points[other])
        columns.append(value)
    return np.stack(columns, axis=1)

X8, w8, D8 = lobatto(8); X4, w4, D4 = lobatto(4); X2, w2, D2 = lobatto(2)
J1 = lagrange(X8, X4)
J2 = lagrange(X4, X2)
K8, K4, K2 = (D.T @ (w[:, None] * D) for D, w in ((D8, w8), (D4, w4), (D2, w2)))
Kd8, Kd4, Kd2 = (np.diag(K) for K in (K8, K4, K2))
f8 = np.array([.5] + [1.]*6 + [.5]); f4 = np.array([.5, 1, 1, .5])
lane = np.arange(128)[None, :]; sub = np.arange(8)[:, None]
ones = np.ones((8, 128))
T = {}
def put(name, a): T[name] = np.ascontiguousarray(np.broadcast_to(a, (8, 128)).astype(np.float32))
kz = lane % 8
K8s = K8 / w8[:, None]
for d in range(1, 8):
    put(f"cy{d}", K8s[sub, (sub - d) % 8] * ones)
for d in range(-7, 8):
    if d == 0: continue
    src = kz - d; ok = (src >= 0) & (src < 8)
    put(f"cz{d}", np.where(ok, K8s[kz, np.clip(src, 0, 7)], 0.0))
put("cyz0", K8s[sub, sub] + K8s[kz, kz])
put("wyz", w8[sub] * w8[kz])
put("mz0", (kz == 0) * 1.0); put("mz7", (kz == 7) * 1.0)
put("jm0", (sub == 0) * 1.0); put("jm7", (sub == 7) * 1.0)
for i in range(4):
    put(f"gk{i}", (Kd8[i] * w8[sub] + w8[i] * Kd8[sub]) * w8[kz] + w8[i] * w8[sub] * Kd8[kz])
    put(f"gw{i}", w8[i] * w8[sub] * w8[kz])
put("m8", f8[sub] * f8[kz])
i4 = sub // 2; jp = sub % 2; h = lane % 2; k4 = (lane % 8) // 2; j4 = 2 * jp + h
for j in range(8):
    for hh in range(2):
        put(f"ry{j}_{hh}", J1[j, 2 * jp + hh] * ones)
RZ = []
for hh in range(2):
    for d in range(-7, 8):
        src = (lane % 8) - d; ok = (src >= 0) & (src < 8) & (h == hh)
        c = np.where(ok, J1[np.clip(src, 0, 7), k4], 0.0)
        if np.any(c != 0): put(f"rz{hh}_{d}", c); RZ.append((hh, d))
PZ = {}
for d in range(-7, 8):
    for hh in range(2):
        src = kz - d; ok = (src >= 0) & (src < 8) & (src % 2 == hh)
        c = np.where(ok, J1[kz, np.clip(src // 2, 0, 3)], 0.0)
        if np.any(c != 0): put(f"pz{hh}_{d}", c); PZ.setdefault(d, []).append(hh)
for b in range(4): put(f"py{b}", J1[sub, b] * ones)
def ops4(tag, M, dirs):
    M = np.asarray(M)
    if "x" in dirs:
        for d in range(4): put(f"{tag}x{d}", M[i4, (i4 - d) % 4] * ones)
    if "y" in dirs:
        put(f"{tag}ya", M[j4, j4]); put(f"{tag}yb", M[j4, 2 * (1 - jp) + h])
        put(f"{tag}yc", M[2 * jp + 1 - h, j4]); put(f"{tag}yd", M[2 * jp + 1 - h, 2 * (1 - jp) + h])
    if "z" in dirs:
        for d in range(-3, 4):
            src = k4 - d; ok = (src >= 0) & (src < 4)
            put(f"{tag}z{d}", np.where(ok, M[k4, np.clip(src, 0, 3)], 0.0))
K4s = K4 / w4[:, None]
for t in ("x", "y", "z"): ops4("a", K4s, t)
put("a0", K4s[i4, i4] + K4s[j4, j4] + K4s[k4, k4])
put("W1", w4[i4] * w4[j4] * w4[k4])
put("G1", Kd4[i4] * w4[j4] * w4[k4] + w4[i4] * Kd4[j4] * w4[k4] + w4[i4] * w4[j4] * Kd4[k4])
put("m1", f4[i4] * f4[j4] * f4[k4])
put("z0", (k4 == 0) * 1.0); put("z3", (k4 == 3) * 1.0)
put("x0", (i4 == 0) * 1.0); put("x3", (i4 == 3) * 1.0)
put("y0", (j4 == 0) * 1.0); put("y3", (j4 == 3) * 1.0)
cor = lambda a: (a == 0) | (a == 3)
cmask = (cor(i4) & cor(j4) & cor(k4)) * 1.0
R2 = np.zeros((4, 4)); R2[0] = J2[:, 0]; R2[3] = J2[:, 1]
P2 = np.zeros((4, 4)); P2[:, 0] = J2[:, 0]; P2[:, 3] = J2[:, 1]
K2s = K2 / w2[:, None]
B2 = np.zeros((4, 4)); B2[np.ix_([0, 3], [0, 3])] = K2s
for t in ("x", "y", "z"):
    ops4("r", R2, t); ops4("p", P2, t); ops4("b", B2, t)
w2e = np.array([w2[0], 0, 0, w2[1]]); Kd2e = np.array([Kd2[0], 0, 0, Kd2[1]])
put("W2", w2e[i4] * w2e[j4] * w2e[k4])
put("G2", Kd2e[i4] * w2e[j4] * w2e[k4] + w2e[i4] * Kd2e[j4] * w2e[k4] + w2e[i4] * w2e[j4] * Kd2e[k4])
put("off2", 1.0 - cmask)
NZ_ = lambda n: np.any(T[n] != 0)
THETA, DELTA = 1.65, 1.35
S_ = THETA / DELTA; rho0 = 1 / S_; rho1 = 1 / (2 * S_ - rho0)
ALPHA = rho1 * rho0; BETA = 2 * rho1 / DELTA

NAMES = [n for n in T if np.any(T[n])]
INDEX = {n: k for k, n in enumerate(NAMES)}
TABLE = np.stack([T[n] for n in NAMES])
K8 = [[float(np.float32(x)) for x in r] for r in K8]
w8 = [float(np.float32(x)) for x in w8]


def live(name):
    return name in INDEX


def lr(v, s):
    return pltpu.roll(v, s % 128, 1)


def sr(v, s):
    return pltpu.roll(v, s % 8, 0)


def halves():
    s = lax.broadcasted_iota(jnp.int32, (8, 128), 0)
    l = lax.broadcasted_iota(jnp.int32, (8, 128), 1)
    return s % 2 == 1, l % 2 == 1

def zops(C, tag, v, skip0=False):
    out = None
    for d in range(-3, 4):
        if (d == 0 and skip0) or not live(f"{tag}z{d}"): continue
        t = C(f"{tag}z{d}") * (lr(v, 2 * d) if d else v)
        out = t if out is None else out + t
    return out

def xops(C, tag, v, skip0=False):
    out = None
    for d in range(4):
        if (d == 0 and skip0) or not live(f"{tag}x{d}"): continue
        t = C(f"{tag}x{d}") * (sr(v, 2 * d) if d else v)
        out = t if out is None else out + t
    return out

def yops(C, tag, v, skip0=False):
    jp1, h1 = halves()
    sw = jnp.where(jp1, sr(v, 1), sr(v, -1)) if live(f"{tag}yb") or live(f"{tag}yd") else None
    def pair(a, b):
        t = None
        if live(a): t = C(a) * v
        if live(b): t = C(b) * sw if t is None else t + C(b) * sw
        return t
    other = pair(f"{tag}yc", f"{tag}yd")
    out = None if other is None else jnp.where(h1, lr(other, 1), lr(other, -1))
    if skip0:
        if live(f"{tag}yb"): out = out + C(f"{tag}yb") * sw
        return out
    same = pair(f"{tag}ya", f"{tag}yb")
    return same if out is None else (out if same is None else out + same)

def a1(C, v, kap, sig):
    k = C("a0") * v + xops(C, "a", v, True) + yops(C, "a", v, True) + zops(C, "a", v, True)
    return C("W1") * (kap * k + sig * v)

def a2(C, v, kap, sig):
    k = xops(C, "b", v) + yops(C, "b", v) + zops(C, "b", v)
    return C("W2") * (kap * k + sig * v)

def restrict2(C, v): return zops(C, "r", yops(C, "r", xops(C, "r", v)))
def prolong2(C, v): return xops(C, "p", yops(C, "p", zops(C, "p", v)))
def sz1(C, v): return v + C("z0") * lr(v, 2) + C("z3") * lr(v, -2)
def xfrom_l(C, v): return C("x0") * sr(v, 2)
def xfrom_r(C, v): return C("x3") * sr(v, -2)
def yfrom_l(C, v): return C("y0") * lr(sr(v, -1), -1)
def yfrom_r(C, v): return C("y3") * lr(sr(v, 1), 1)

def a_fine(C, v, c1, rho):
    e = C("cyz0") + rho
    out = []
    for i in range(8):
        t = e * v[i]
        for d in range(1, 8): t = t + C(f"cy{d}") * sr(v[i], d)
        for d in range(-7, 8):
            if d: t = t + C(f"cz{d}") * lr(v[i], d)
        x = K8[i][0] * v[0]
        for a in range(1, 8): x = x + K8[i][a] * v[a]
        out.append(c1 * (x + w8[i] * t))
    return out

def sz8(C, v): return v + C("mz0") * lr(v, 1) + C("mz7") * lr(v, -1)

MESH = pl.DeviceIdType.MESH
NY = 4
ZR = 32
YR = 4
GX = ZR * YR * 2
R = 5
NC = (2 * R + 1) * NY
OWN = R * NY
PARTNERS = [(dx, dy) for dx in range(-R, R + 1) for dy in range(NY) if (dx, dy) != (0, 0)]
ROUNDS = 7
TI = 1.0 / THETA


def slot(dx, dy):
    return (dx + R) * NY + dy % NY


def kernel(tab_hbm, forc, kap_in, sig_in, one_hot, sol, res, rel,
           tab, V, ks_s, KS, SX, SY, SC, RX, RY, RC, ID0, B, D0, R1, Q, XS,
           us, U, ID1, ID2, C1B, D0B, VA, R1B, D1B, VB, C2B, G0B, QB, VC, X1,
           ap, AZ, pp, AP,
           tab_sem, ks_send, ks_recv, f_send, f_recv, u_send, u_recv,
           z_send, z_recv, p_send, p_recv, chain):
    gx = lax.axis_index("gx")
    gy = lax.axis_index("gy")
    core = lax.rem(gx, 2)
    zc = lax.rem(gx // 2, ZR)
    yc = gx // (2 * ZR)

    def at(dx, dy):
        return (lax.rem(gx + dx + GX, GX), lax.rem(gy + dy + NY, NY))

    def zring(k):
        return (yc * (2 * ZR) + 2 * lax.rem(zc + k + ZR, ZR) + core, gy)

    def plane(dy, dc, dx):
        return (lax.rem(yc + dy, YR) * (2 * ZR) + 2 * zc + lax.rem(core + dc, 2), lax.rem(gy + dx, NY))

    def C(name):
        return tab[INDEX[name]]

    tab_copy = pltpu.make_async_copy(tab_hbm, tab, tab_sem)
    tab_copy.start()

    barrier = pltpu.get_barrier_semaphore()
    greet = [at(dx, dy) for dx, dy in PARTNERS]
    greet += [zring(k) for k in (-3, -2, -1, 1, 2, 3)] + [plane(k, 0, 0) for k in (1, 2, 3)]
    for d in greet:
        pl.semaphore_signal(barrier, inc=1, device_id=d, device_id_type=MESH)

    hot = one_hot[...]
    def lanes(ref):
        return jnp.dot(jnp.broadcast_to(ref[...], (8, 16)), hot, precision=lax.Precision.HIGHEST, preferred_element_type=jnp.float32)
    kap = lanes(kap_in)
    sig = lanes(sig_in)
    ks_s[0:1] = kap[0:1]
    ks_s[1:2] = sig[0:1]
    KS[OWN, 0:1] = kap[0:1]
    KS[OWN, 1:2] = sig[0:1]
    tab_copy.wait()

    def put_faces(rnd):
        SX[rnd, 0] = V[0:8]
        SX[rnd, 1] = V[56:64]
        SY[rnd, 0] = V[pl.ds(0, 8, stride=8)]
        SY[rnd, 1] = V[pl.ds(7, 8, stride=8)]
        for k, row in enumerate((0, 7, 56, 63)):
            SC[rnd, k] = V[row:row + 1]

    def face_copies(rnd):
        out = []
        for s in range(2):
            step = 2 * s - 1
            out.append((SX.at[rnd, s], RX.at[rnd, 1 - s], at(step, 0)))
        for s in range(2):
            step = 2 * s - 1
            out.append((SY.at[rnd, s], RY.at[rnd, 1 - s], at(0, step)))
        for k in range(4):
            out.append((SC.at[rnd, k], RC.at[rnd, 3 - k], at(2 * (k // 2) - 1, 2 * (k % 2) - 1)))
        return [pltpu.make_async_remote_copy(src_ref=a, dst_ref=b, send_sem=f_send.at[rnd, n], recv_sem=f_recv.at[rnd, RSEM[n]],
                                             device_id=d, device_id_type=MESH) for n, (a, b, d) in enumerate(out)]

    def face_start(rnd, tiles):
        for i in range(8):
            V[8 * i:8 * i + 8] = tiles[i]
        put_faces(rnd)
        for c in face_copies(rnd):
            c.start()

    def face_wait(rnd):
        for n in range(8):
            pltpu.make_async_remote_copy(src_ref=(RX.at[rnd, n] if n < 2 else RY.at[rnd, n - 2] if n < 4 else RC.at[rnd, n - 4]),
                                         dst_ref=(RX.at[rnd, n] if n < 2 else RY.at[rnd, n - 2] if n < 4 else RC.at[rnd, n - 4]),
                                         send_sem=f_send.at[rnd, n], recv_sem=f_recv.at[rnd, n], device_id=at(1, 0), device_id_type=MESH).wait_recv()
        V[0:8] = V[0:8] + RX[rnd, 0]
        V[56:64] = V[56:64] + RX[rnd, 1]
        V[pl.ds(0, 8, stride=8)] = V[pl.ds(0, 8, stride=8)] + RY[rnd, 0]
        V[pl.ds(7, 8, stride=8)] = V[pl.ds(7, 8, stride=8)] + RY[rnd, 1]
        for k, row in enumerate((0, 7, 56, 63)):
            V[row:row + 1] = V[row:row + 1] + RC[rnd, k]
        return [V[8 * i:8 * i + 8] for i in range(8)]

    pl.semaphore_wait(barrier, len(greet))

    face_start(0, [sz8(C, forc[i]) for i in range(8)])
    def ks_copy(dx, dy):
        return pltpu.make_async_remote_copy(src_ref=ks_s, dst_ref=KS.at[slot(-dx, -dy)], send_sem=ks_send, recv_sem=ks_recv,
                                            device_id=at(dx, dy), device_id_type=MESH)
    for dx, dy in PARTNERS:
        ks_copy(dx, dy).start()
    for k in (-3, 3):
        pl.semaphore_signal(chain.at[0], inc=1, device_id=zring(k), device_id_type=MESH)
    for k in (1, 2, 3):
        pl.semaphore_signal(chain.at[3], inc=1, device_id=plane(k, 0, 0), device_id_type=MESH)

    def all_but_one(buf, send, recv):
        return pltpu.make_async_remote_copy(src_ref=buf.at[pl.ds(0, NC - 1)], dst_ref=buf.at[pl.ds(0, NC - 1)], send_sem=send, recv_sem=recv,
                                            device_id=at(1, 0), device_id_type=MESH)

    b = face_wait(0)
    for i in range(8):
        B[i] = b[i]
        R1[i] = b[i]
        XS[i] = jnp.zeros((8, 128), jnp.float32)
    all_but_one(KS, ks_send, ks_recv).wait_recv()

    def row(dx, dy, which):
        return KS[slot(dx, dy), which:which + 1]
    prof = [[], []]
    for dx in (-1, 0, 1):
        for which in range(2):
            prof[which].append(row(dx, 0, which) + C("jm0") * row(dx, -1, which) + C("jm7") * row(dx, 1, which))
    for i in range(8):
        kk, ss = prof[0][1], prof[1][1]
        if i == 0:
            kk, ss = kk + prof[0][0], ss + prof[1][0]
        if i == 7:
            kk, ss = kk + prof[0][2], ss + prof[1][2]
        ii = min(i, 7 - i)
        ID0[i] = 1.0 / sz8(C, kk * C(f"gk{ii}") + ss * C(f"gw{ii}"))

    def kap_of(dx, dy):
        return KS[(dx + R) * NY + dy, 0:1]

    def sig_of(dx, dy):
        return KS[(dx + R) * NY + dy, 1:2]

    def assembled(buf, dx):
        base = (dx + R) * NY
        u = [buf[base + dy] + xfrom_l(C, buf[base - NY + dy]) + xfrom_r(C, buf[base + NY + dy]) for dy in range(NY)]
        up = [yfrom_l(C, u[dy]) for dy in range(NY)]
        dn = [yfrom_r(C, u[dy]) for dy in range(NY)]
        return [u[dy] + up[(dy - 1) % NY] + dn[(dy + 1) % NY] for dy in range(NY)]

    def over(radius, body):
        def go(n, carry):
            body(n - radius)
            return carry
        lax.fori_loop(0, 2 * radius + 1, go, 0)

    def g_one(dx):
        for dy in range(NY):
            c = (dx + R) * NY + dy
            VA[c] = sz1(C, kap_of(dx, dy) * C("G1") + sig_of(dx, dy) * C("W1"))
            VB[c] = sz1(C, kap_of(dx, dy) * C("G2") + sig_of(dx, dy) * C("W2"))
    over(R, g_one)
    def g_two(dx):
        s1, s2 = assembled(VA, dx), assembled(VB, dx)
        for dy in range(NY):
            c = (dx + R) * NY + dy
            ID1[c] = 1.0 / s1[dy]
            ID2[c] = 1.0 / (s2[dy] + C("off2"))
    over(R - 1, g_two)

    pl.semaphore_wait(chain.at[0], 2)
    for k in (-6, 6):
        pl.semaphore_signal(chain.at[1], inc=1, device_id=zring(k), device_id_type=MESH)

    c1 = kap * C("wyz")
    rho = sig / kap

    def tiles(ref):
        return [ref[i] for i in range(8)]

    def u_copy(cyc, dx, dy):
        return pltpu.make_async_remote_copy(src_ref=us.at[cyc], dst_ref=U.at[cyc, slot(-dx, -dy)], send_sem=u_send.at[cyc], recv_sem=u_recv.at[cyc],
                                            device_id=at(dx, dy), device_id_type=MESH)

    def coarse(cyc):
        Uc = U.at[cyc]
        def first(dx):
            s = assembled(Uc, dx)
            for dy in range(NY):
                c = (dx + R) * NY + dy
                d0 = TI * s[dy] * ID1[c]
                C1B[c] = s[dy]
                D0B[c] = d0
                VA[c] = sz1(C, a1(C, d0, kap_of(dx, dy), sig_of(dx, dy)))
        over(R - 1, first)
        def second(dx):
            s = assembled(VA, dx)
            for dy in range(NY):
                c = (dx + R) * NY + dy
                r1 = C1B[c] - s[dy]
                d1 = ALPHA * D0B[c] + BETA * r1 * ID1[c]
                t = C("m1") * r1 - a1(C, d1, kap_of(dx, dy), sig_of(dx, dy))
                R1B[c] = r1
                D1B[c] = d1
                VB[c] = sz1(C, restrict2(C, t))
        over(R - 2, second)
        def third(dx):
            s = assembled(VB, dx)
            for dy in range(NY):
                c = (dx + R) * NY + dy
                g0 = TI * s[dy] * ID2[c]
                C2B[c] = s[dy]
                G0B[c] = g0
                VA[c] = sz1(C, a2(C, g0, kap_of(dx, dy), sig_of(dx, dy)))
        over(R - 3, third)
        def fourth(dx):
            s = assembled(VA, dx)
            for dy in range(NY):
                c = (dx + R) * NY + dy
                x2 = (1.0 + ALPHA) * G0B[c] + BETA * (C2B[c] - s[dy]) * ID2[c]
                q = D1B[c] + prolong2(C, x2)
                QB[c] = q
                VC[c] = sz1(C, a1(C, q, kap_of(dx, dy), sig_of(dx, dy)))
        over(R - 4, fourth)
        s = assembled(VC, 0)
        for dy in range(1):
            c = OWN + dy
            X1[dy] = D0B[c] + QB[c] + TI * (R1B[c] - s[dy]) * ID1[c]

    def restrict1(t):
        xs = [sum(float(J1[i, a]) * t[i] for i in range(8)) for a in range(4)]
        for s in range(8):
            V[8 * s:8 * s + 8] = xs[s // 2]
        out = None
        for hh in range(2):
            y = None
            for j in range(8):
                if live(f"ry{j}_{hh}"):
                    p = C(f"ry{j}_{hh}") * V[pl.ds(j, 8, stride=8)]
                    y = p if y is None else y + p
            for h2, d in RZ:
                if h2 == hh:
                    p = C(f"rz{hh}_{d}") * (lr(y, d) if d else y)
                    out = p if out is None else out + p
        return out

    def prolong1(e):
        z = [None, None]
        for d in PZ:
            r = lr(e, d) if d else e
            for hh in PZ[d]:
                p = C(f"pz{hh}_{d}") * r
                z[hh] = p if z[hh] is None else z[hh] + p
        V[0:8] = z[0]
        V[8:16] = z[1]
        ex = []
        for a in range(4):
            ex.append(sum(C(f"py{bb}") * V[pl.ds((bb % 2) * 8 + 2 * a + bb // 2, 8, stride=0)] for bb in range(4)))
        return [sum(float(J1[i, a]) * ex[a] for a in range(4)) for i in range(8)]

    def apply(rnd, v):
        face_start(rnd, [sz8(C, t) for t in a_fine(C, v, c1, rho)])
        return face_wait(rnd)

    def cycle(cyc, carry):
        rnd = 1 + 3 * cyc
        r = tiles(R1)
        d0 = [TI * r[i] * ID0[i] for i in range(8)]
        for i in range(8):
            D0[i] = d0[i]
        s = apply(rnd, d0)
        d1, t = [], []
        for i in range(8):
            r1 = R1[i] - s[i]
            R1[i] = r1
            d1.append(ALPHA * D0[i] + BETA * r1 * ID0[i])
            Q[i] = d1[i]
        w = a_fine(C, d1, c1, rho)
        t = [float(f8[i]) * C("m8") * R1[i] - w[i] for i in range(8)]
        u = sz1(C, restrict1(t))
        us[cyc] = u
        U[cyc, OWN] = u
        for dx, dy in PARTNERS:
            u_copy(cyc, dx, dy).start()
        @pl.when(cyc == 0)
        def _():
            pl.semaphore_wait(chain.at[1], 2)
            for k in (-10, 10):
                pl.semaphore_signal(chain.at[2], inc=1, device_id=zring(k), device_id_type=MESH)
        all_but_one(U.at[cyc], u_send.at[cyc], u_recv.at[cyc]).wait_recv()
        coarse(cyc)
        e = prolong1(X1[0])
        q = [Q[i] + e[i] for i in range(8)]
        for i in range(8):
            Q[i] = q[i]
        s = apply(rnd + 1, q)
        dl = []
        for i in range(8):
            r3 = R1[i] - s[i]
            R1[i] = r3
            x = TI * r3 * ID0[i]
            dl.append(x)
            XS[i] = XS[i] + (D0[i] + Q[i] + x)
        s = apply(rnd + 2, dl)
        for i in range(8):
            R1[i] = R1[i] - s[i]
        return carry

    lax.fori_loop(0, 2, cycle, 0)

    def dot(p, q):
        t = sum(float(f8[i]) * C("m8") * p[i] * q[i] for i in range(8))
        return jnp.sum(jnp.sum(t, axis=1, keepdims=True), axis=0, keepdims=True)
    ln = lax.broadcasted_iota(jnp.int32, (1, 128), 1)
    mine = jnp.where(ln == 0, dot(B, B), jnp.where(ln == 1, dot(B, R1), dot(R1, R1)))
    ap[...] = mine
    AZ[zc] = mine
    pl.semaphore_wait(chain.at[2], 2)
    pl.semaphore_wait(chain.at[3], 3)
    def z_copy(k):
        return pltpu.make_async_remote_copy(src_ref=ap, dst_ref=AZ.at[zc], send_sem=z_send, recv_sem=z_recv, device_id=zring(k), device_id_type=MESH)
    for k in range(1, ZR // 2):
        z_copy(k).start()
        z_copy(-k).start()
    z_copy(ZR // 2).start()
    def most(buf, send, recv):
        return pltpu.make_async_remote_copy(src_ref=buf.at[pl.ds(0, 31)], dst_ref=buf.at[pl.ds(0, 31)], send_sem=send, recv_sem=recv,
                                            device_id=at(1, 0), device_id_type=MESH)
    most(AZ, z_send, z_recv).wait_recv()
    part = AZ[0]
    for k in range(1, ZR):
        part = part + AZ[k]
    pp[...] = part
    pi = yc * 8 + gy * 2 + core
    AP[pi] = part
    others = [(a, c, x) for a in range(YR) for c in range(2) for x in range(NY) if (a, c, x) != (0, 0, 0)]
    def p_copy(o):
        return pltpu.make_async_remote_copy(src_ref=pp, dst_ref=AP.at[pi], send_sem=p_send, recv_sem=p_recv, device_id=plane(*o), device_id_type=MESH)
    for o in others:
        p_copy(o).start()
    most(AP, p_send, p_recv).wait_recv()
    tot = AP[0]
    for k in range(1, 32):
        tot = tot + AP[k]
    bb, br, rr = tot[0:1, 0:1], tot[0:1, 1:2], tot[0:1, 2:3]
    ww = bb - 2.0 * br + rr
    coef = (bb - br) / ww
    for i in range(8):
        sol[i] = coef * XS[i]
        res[i] = B[i] - coef * (B[i] - R1[i])
    rel[...] = jnp.broadcast_to(jnp.sqrt((bb * rr - br * br) / (ww * bb)), (1, 128))

    most(AP, p_send, p_recv).wait_send()
    most(AZ, z_send, z_recv).wait_send()
    all_but_one(KS, ks_send, ks_recv).wait_send()
    for cyc in range(2):
        all_but_one(U.at[cyc], u_send.at[cyc], u_recv.at[cyc]).wait_send()
    for rnd in range(ROUNDS):
        for c in face_copies(rnd):
            c.wait_send()


RSEM = [1, 0, 3, 2, 7, 6, 5, 4]


def solution(mesh):
    f32 = jnp.float32
    col = pltpu.VMEM((NC, 8, 128), f32)
    fine = pltpu.VMEM((8, 8, 128), f32)
    row = pltpu.VMEM((1, 128), f32)
    scratch = [
        pltpu.VMEM((len(NAMES), 8, 128), f32), pltpu.VMEM((64, 128), f32),
        pltpu.VMEM((2, 128), f32), pltpu.VMEM((NC, 2, 128), f32),
        pltpu.VMEM((ROUNDS, 2, 8, 128), f32), pltpu.VMEM((ROUNDS, 2, 8, 128), f32), pltpu.VMEM((ROUNDS, 4, 1, 128), f32),
        pltpu.VMEM((ROUNDS, 2, 8, 128), f32), pltpu.VMEM((ROUNDS, 2, 8, 128), f32), pltpu.VMEM((ROUNDS, 4, 1, 128), f32),
        fine, fine, fine, fine, fine, fine,
        pltpu.VMEM((2, 8, 128), f32), pltpu.VMEM((2, NC, 8, 128), f32),
        col, col, col, col, col, col, col, col, col, col, col, col, pltpu.VMEM((NY, 8, 128), f32),
        row, pltpu.VMEM((32, 1, 128), f32), row, pltpu.VMEM((32, 1, 128), f32),
        pltpu.SemaphoreType.DMA, pltpu.SemaphoreType.DMA, pltpu.SemaphoreType.DMA,
        pltpu.SemaphoreType.DMA((ROUNDS, 8)), pltpu.SemaphoreType.DMA((ROUNDS, 8)),
        pltpu.SemaphoreType.DMA((2,)), pltpu.SemaphoreType.DMA((2,)),
        pltpu.SemaphoreType.DMA, pltpu.SemaphoreType.DMA, pltpu.SemaphoreType.DMA, pltpu.SemaphoreType.DMA,
        pltpu.SemaphoreType.REGULAR((4,)),
    ]
    vm = pl.BlockSpec(memory_space=pltpu.VMEM)
    call = pl.pallas_call(
        kernel,
        out_shape=[jax.ShapeDtypeStruct((8, 8, 128), f32), jax.ShapeDtypeStruct((8, 8, 128), f32), jax.ShapeDtypeStruct((1, 128), f32)],
        in_specs=[pl.BlockSpec(memory_space=pl.ANY), vm, vm, vm, vm],
        out_specs=[vm, vm, vm],
        scratch_shapes=scratch,
        compiler_params=pltpu.CompilerParams(collective_id=0, has_side_effects=True),
        name="helmholtz",
    )
    hot = (np.arange(128)[None, :] // 8 == np.arange(16)[:, None]).astype(np.float32)

    def local(forcing, kappa, sigma):
        s, r, e = call(jnp.asarray(TABLE), forcing, kappa.reshape(1, 16), sigma.reshape(1, 16), jnp.asarray(hot))
        return s, r, e[0, 0]

    return jax.shard_map(local, mesh=mesh, in_specs=(P("gx", "gy", None),) * 3,
                         out_specs=(P("gx", "gy", None), P("gx", "gy", None), P()), check_vma=False)
```

time: 653 us -> 109 us (0.17); the launches traced: 643 us -> 109 us
  starting transfers between devices: 414 us -> 0 us
  Pallas kernels: 0 us -> 105 us
  blocking collectives: 80.8 us -> 0 us
  matrix products: 62.1 us -> 0 us
  local copies, waits for them, and re-layouts: 41 us -> 2.06 us
  waiting for transfers between devices: 22.7 us -> 0 us
  other arithmetic: 12.4 us -> 0 us
  between operations: 10.1 us -> 1.81 us
    ppermute x96 -> x0, starting transfers between devices: 414 us -> none  [the longest x48 296 us: with_halo(): lax.ppermute(head, axis, [((i + 1) % count, i) for i in range(count)])]
    pallas_call x0 -> x1, Pallas kernels: none -> 105 us  [local(): call(jnp.asarray(TABLE), forcing, kappa.reshape(1, 16), sigma.reshape(1,...]
    psum x4 -> x0, blocking collectives: 80.8 us -> none  [one_axis_at_a_time(): return functools.reduce(lax.psum, axes, shard)]
    dot_general x120 -> x0, matrix products: 62.1 us -> none  [the longest x16 28.2 us: element_apply(): third = jnp.einsum('ak,eifjgk->eifjga', deriv, block, precision=high)]
    ppermute x96 -> x0, waiting for transfers between devices: 22.7 us -> none  [the longest x48 22.6 us: with_halo(): lax.ppermute(head, axis, [((i + 1) % count, i) for i in range(count)])]
    slice x184 -> x0, local copies, waits for them, and re-layouts: 13.1 us -> none  [the longest x80 5.43 us: with_halo(): lax.slice_in_dim(cells, cells.shape[dim] - width, cells.shape[dim], axis=...]
    another operation x54 -> x0, local copies, waits for them, and re-layouts: 9.15 us -> none
    reshape x48 -> x0, local copies, waits for them, and re-layouts: 8.54 us -> none  [the longest x24 4.53 us: element_apply(): block = field.reshape(ex, count, ey, count, ez, count)]
  transfers between devices with their start and end apart: 96 -> 0, of which waited for: 39 -> 0; matrix products, arithmetic and copies ran while one was open for 7% -> 0% of each run, Pallas kernels for 0% -> 0%
where the time goes in v1:
time: 109 us
  Pallas kernels  105 us (96%)
  local copies, waits for them, and re-layouts  2.06 us (2%)
  between operations  1.81 us (2%)
    pallas_call x1, Pallas kernels, local(): call(jnp.asarray(TABLE), forcing, kappa.reshape(1, 16), sigma.reshape(1,...  105 us

profile of v1, /device:TPU:1, one launch (start us, length us, event | category | flops | bytes accessed | tf_op | source)
XLA Modules:
  0.0 108.8 jit_solution(12614167965122155769)
XLA Ops:
  0.6 104.9 %helmholtz.1 = (f32[8,8,128]{2,1,0:T(8,128)}, f32[8,8,128]{2,1,0:T(8,128)}, f32[1,128]{1,0:T(1,128)}) custom-call(f32[162,8,128]{2,1,0:T(8,128)} %constant.4.clone.tab_hbm, f32[8,8,128]{2,1,0:T(8,128)} %forc.1, f32[1,16]{1,0:T(1,128)} %bitcast.4, f32[1,16]{1,0:T(1,128)} %bitcast.5, f32[16,128]{1,0:T(8,128)} %constant.5.clone.one_hot), custom_call_target="tpu_custom_call" | custom-call | tf_op jit(solution)/shard_map/helmholtz/pallas_call | solution.py:611
  105.6 0.0 copy-start
  105.6 1.4 %copy.11 = f32[8,8,128]{2,1,0:T(8,128)} copy(f32[8,8,128]{2,1,0:T(8,128)} %get-tuple-element.12) | data formatting | bytes 65536
  107.0 0.0 copy-done
  107.0 0.0 copy-start.1
  107.0 0.6 copy.12
  107.6 0.1 copy-done.1
Async XLA Ops:
  105.6 1.4 %copy-start = (f32[8,8,128]{2,1,0:T(8,128)S(1)}, f32[8,8,128]{2,1,0:T(8,128)}, u32[]{:S(2)}) copy-start(f32[8,8,128]{2,1,0:T(8,128)} %get-tuple-element.13) | copy-start | bytes 98308
  107.0 0.7 copy-start.1

commit v2 on v1

--- a/solution.py
+++ b/solution.py
@@ -1,3 +1,5 @@
+import contextlib
+
 import jax
 import jax.numpy as jnp
 import numpy as np
@@ -114,6 +116,23 @@
 put("W2", w2e[i4] * w2e[j4] * w2e[k4])
 put("G2", Kd2e[i4] * w2e[j4] * w2e[k4] + w2e[i4] * Kd2e[j4] * w2e[k4] + w2e[i4] * w2e[j4] * Kd2e[k4])
 put("off2", 1.0 - cmask)
+KJ = K8s @ J1
+KJx = K8 @ J1
+for d in range(-7, 8):
+    for hh in range(2):
+        src = kz - d; ok = (src >= 0) & (src < 8) & (src % 2 == hh)
+        put(f"qz{hh}_{d}", np.where(ok, KJ[kz, np.clip(src // 2, 0, 3)], 0.0))
+for b in range(4): put(f"qy{b}", KJ[sub, b] * ones)
+for j0 in (0, 7):
+    for hh in range(2): put(f"fy{j0}_{hh}", KJ[j0, 2 * jp + hh] * ones)
+for i0 in (0, 7):
+    for j0 in (0, 7):
+        a0, b0 = (0 if i0 == 0 else 3), (0 if j0 == 0 else 3)
+        for hh in range(2):
+            b_ = 2 * jp + hh
+            put(f"fc{i0}{j0}_{hh}", (KJ[i0, i4] * (b_ == b0) + KJ[j0, b_] * (i4 == a0)) * ones)
+        put(f"fo{i0}{j0}", ((i4 == a0) & (jp == b0 // 2)) * ones)
+for q in range(2): put(f"hot{q}", (lane // 8 == sub + 8 * q) * 1.0)
 NZ_ = lambda n: np.any(T[n] != 0)
 THETA, DELTA = 1.65, 1.35
 S_ = THETA / DELTA; rho0 = 1 / S_; rho1 = 1 / (2 * S_ - rho0)
@@ -206,12 +225,17 @@
 
 def sz8(C, v): return v + C("mz0") * lr(v, 1) + C("mz7") * lr(v, -1)
 
+
+def scope(name):
+    return contextlib.nullcontext()
+
+
 MESH = pl.DeviceIdType.MESH
 NY = 4
 ZR = 32
 YR = 4
 GX = ZR * YR * 2
-R = 5
+R = 6
 NC = (2 * R + 1) * NY
 OWN = R * NY
 PARTNERS = [(dx, dy) for dx in range(-R, R + 1) for dy in range(NY) if (dx, dy) != (0, 0)]
@@ -223,11 +247,11 @@
     return (dx + R) * NY + dy % NY
 
 
-def kernel(tab_hbm, forc, kap_in, sig_in, one_hot, sol, res, rel,
-           tab, V, ks_s, KS, SX, SY, SC, RX, RY, RC, ID0, B, D0, R1, Q, XS,
-           us, U, ID1, ID2, C1B, D0B, VA, R1B, D1B, VB, C2B, G0B, QB, VC, X1,
+def kernel(tab_hbm, forc_hbm, kap_hbm, sig_hbm, z_out, b_out, r_out, scal,
+           tab, forc, kap_in, sig_in, V, ks_s, KS, SX, SY, SC, RX, RY, RC, ID0, B, D0, R1, Q, XS,
+           us, U, ID1, ID2, C1B, D0B, VA, R1B, D1B, VB, C2B, G0B, QB, VC, X1, TMP, Z,
            ap, AZ, pp, AP,
-           tab_sem, ks_send, ks_recv, f_send, f_recv, u_send, u_recv,
+           in_sem, out_sem, ks_send, kf_send, kf_recv, ks_recv, f_send, f_recv, u_send, u_recv,
            z_send, z_recv, p_send, p_recv, chain):
     gx = lax.axis_index("gx")
     gy = lax.axis_index("gy")
@@ -247,16 +271,19 @@
     def C(name):
         return tab[INDEX[name]]
 
-    tab_copy = pltpu.make_async_copy(tab_hbm, tab, tab_sem)
-    tab_copy.start()
-
+    loads = [pltpu.make_async_copy(a, b, in_sem.at[k]) for k, (a, b) in enumerate(((kap_hbm, kap_in), (sig_hbm, sig_in), (tab_hbm, tab), (forc_hbm, forc)))]
+    for c in loads:
+        c.start()
     barrier = pltpu.get_barrier_semaphore()
     greet = [at(dx, dy) for dx, dy in PARTNERS]
     greet += [zring(k) for k in (-3, -2, -1, 1, 2, 3)] + [plane(k, 0, 0) for k in (1, 2, 3)]
     for d in greet:
         pl.semaphore_signal(barrier, inc=1, device_id=d, device_id_type=MESH)
 
-    hot = one_hot[...]
+    with scope('tab_wait'):
+        for c in loads:
+            c.wait()
+    hot = jnp.concatenate([C("hot0"), C("hot1")], axis=0)
     def lanes(ref):
         return jnp.dot(jnp.broadcast_to(ref[...], (8, 16)), hot, precision=lax.Precision.HIGHEST, preferred_element_type=jnp.float32)
     kap = lanes(kap_in)
@@ -265,7 +292,6 @@
     ks_s[1:2] = sig[0:1]
     KS[OWN, 0:1] = kap[0:1]
     KS[OWN, 1:2] = sig[0:1]
-    tab_copy.wait()
 
     def put_faces(rnd):
         SX[rnd, 0] = V[0:8]
@@ -292,14 +318,16 @@
         for i in range(8):
             V[8 * i:8 * i + 8] = tiles[i]
         put_faces(rnd)
-        for c in face_copies(rnd):
-            c.start()
+        with scope('face_start'):
+            for c in face_copies(rnd):
+                c.start()
 
     def face_wait(rnd):
-        for n in range(8):
-            pltpu.make_async_remote_copy(src_ref=(RX.at[rnd, n] if n < 2 else RY.at[rnd, n - 2] if n < 4 else RC.at[rnd, n - 4]),
-                                         dst_ref=(RX.at[rnd, n] if n < 2 else RY.at[rnd, n - 2] if n < 4 else RC.at[rnd, n - 4]),
-                                         send_sem=f_send.at[rnd, n], recv_sem=f_recv.at[rnd, n], device_id=at(1, 0), device_id_type=MESH).wait_recv()
+        with scope('face_wait'):
+            for n in range(8):
+                pltpu.make_async_remote_copy(src_ref=(RX.at[rnd, n] if n < 2 else RY.at[rnd, n - 2] if n < 4 else RC.at[rnd, n - 4]),
+                                             dst_ref=(RX.at[rnd, n] if n < 2 else RY.at[rnd, n - 2] if n < 4 else RC.at[rnd, n - 4]),
+                                             send_sem=f_send.at[rnd, n], recv_sem=f_recv.at[rnd, n], device_id=at(1, 0), device_id_type=MESH).wait_recv()
         V[0:8] = V[0:8] + RX[rnd, 0]
         V[56:64] = V[56:64] + RX[rnd, 1]
         V[pl.ds(0, 8, stride=8)] = V[pl.ds(0, 8, stride=8)] + RY[rnd, 0]
@@ -308,29 +336,33 @@
             V[row:row + 1] = V[row:row + 1] + RC[rnd, k]
         return [V[8 * i:8 * i + 8] for i in range(8)]
 
-    pl.semaphore_wait(barrier, len(greet))
-
-    face_start(0, [sz8(C, forc[i]) for i in range(8)])
+    first_v = [sz8(C, forc[i]) for i in range(8)]
+    with scope('barrier'):
+        pl.semaphore_wait(barrier, len(greet))
+
     def ks_copy(dx, dy):
-        return pltpu.make_async_remote_copy(src_ref=ks_s, dst_ref=KS.at[slot(-dx, -dy)], send_sem=ks_send, recv_sem=ks_recv,
-                                            device_id=at(dx, dy), device_id_type=MESH)
-    for dx, dy in PARTNERS:
-        ks_copy(dx, dy).start()
+        near = abs(dx) <= 1 and dy != 2
+        return pltpu.make_async_remote_copy(src_ref=ks_s, dst_ref=KS.at[slot(-dx, -dy)], send_sem=ks_send if near else kf_send,
+                                            recv_sem=ks_recv if near else kf_recv, device_id=at(dx, dy), device_id_type=MESH)
+    near = [(dx, dy) for dx, dy in PARTNERS if abs(dx) <= 1 and dy != 2]
+    far = [p for p in PARTNERS if p not in near]
+    for p in near:
+        ks_copy(*p).start()
+    face_start(0, first_v)
+    with scope('ks_send'):
+        for p in far:
+            ks_copy(*p).start()
     for k in (-3, 3):
         pl.semaphore_signal(chain.at[0], inc=1, device_id=zring(k), device_id_type=MESH)
     for k in (1, 2, 3):
         pl.semaphore_signal(chain.at[3], inc=1, device_id=plane(k, 0, 0), device_id_type=MESH)
 
-    def all_but_one(buf, send, recv):
-        return pltpu.make_async_remote_copy(src_ref=buf.at[pl.ds(0, NC - 1)], dst_ref=buf.at[pl.ds(0, NC - 1)], send_sem=send, recv_sem=recv,
+    def landed(buf, count, send, recv):
+        return pltpu.make_async_remote_copy(src_ref=buf.at[pl.ds(0, count)], dst_ref=buf.at[pl.ds(0, count)], send_sem=send, recv_sem=recv,
                                             device_id=at(1, 0), device_id_type=MESH)
 
-    b = face_wait(0)
-    for i in range(8):
-        B[i] = b[i]
-        R1[i] = b[i]
-        XS[i] = jnp.zeros((8, 128), jnp.float32)
-    all_but_one(KS, ks_send, ks_recv).wait_recv()
+    with scope('ks_wait'):
+        landed(KS, len(near), ks_send, ks_recv).wait_recv()
 
     def row(dx, dy, which):
         return KS[slot(dx, dy), which:which + 1]
@@ -347,6 +379,12 @@
         ii = min(i, 7 - i)
         ID0[i] = 1.0 / sz8(C, kk * C(f"gk{ii}") + ss * C(f"gw{ii}"))
 
+    b = face_wait(0)
+    for i in range(8):
+        B[i] = b[i]
+        R1[i] = b[i]
+        XS[i] = jnp.zeros((8, 128), jnp.float32)
+
     def kap_of(dx, dy):
         return KS[(dx + R) * NY + dy, 0:1]
 
@@ -361,24 +399,27 @@
         return [u[dy] + up[(dy - 1) % NY] + dn[(dy + 1) % NY] for dy in range(NY)]
 
     def over(radius, body):
-        def go(n, carry):
-            body(n - radius)
-            return carry
-        lax.fori_loop(0, 2 * radius + 1, go, 0)
-
-    def g_one(dx):
-        for dy in range(NY):
-            c = (dx + R) * NY + dy
-            VA[c] = sz1(C, kap_of(dx, dy) * C("G1") + sig_of(dx, dy) * C("W1"))
-            VB[c] = sz1(C, kap_of(dx, dy) * C("G2") + sig_of(dx, dy) * C("W2"))
-    over(R, g_one)
-    def g_two(dx):
-        s1, s2 = assembled(VA, dx), assembled(VB, dx)
-        for dy in range(NY):
-            c = (dx + R) * NY + dy
-            ID1[c] = 1.0 / s1[dy]
-            ID2[c] = 1.0 / (s2[dy] + C("off2"))
-    over(R - 1, g_two)
+        for dx in range(-radius, radius + 1):
+            body(dx)
+
+    def coarse_diagonals():
+        with scope('kf_wait'):
+            landed(KS, len(far), kf_send, kf_recv).wait_recv()
+        def g_one(dx):
+            for dy in range(NY):
+                c = (dx + R) * NY + dy
+                VA[c] = sz1(C, kap_of(dx, dy) * C("G1") + sig_of(dx, dy) * C("W1"))
+                VB[c] = sz1(C, kap_of(dx, dy) * C("G2") + sig_of(dx, dy) * C("W2"))
+        with scope('g_one'):
+            over(R, g_one)
+        def g_two(dx):
+            s1, s2 = assembled(VA, dx), assembled(VB, dx)
+            for dy in range(NY):
+                c = (dx + R) * NY + dy
+                ID1[c] = 1.0 / s1[dy]
+                ID2[c] = 1.0 / (s2[dy] + C("off2"))
+        with scope('g_two'):
+            over(R - 1, g_two)
 
     pl.semaphore_wait(chain.at[0], 2)
     for k in (-6, 6):
@@ -394,50 +435,61 @@
         return pltpu.make_async_remote_copy(src_ref=us.at[cyc], dst_ref=U.at[cyc, slot(-dx, -dy)], send_sem=u_send.at[cyc], recv_sem=u_recv.at[cyc],
                                             device_id=at(dx, dy), device_id_type=MESH)
 
+    def columns(radius):
+        return [(dx, dy, (dx + R) * NY + dy) for dx in range(-radius, radius + 1) for dy in range(NY)]
+
+    def sums(buf, radius, put):
+        for dx in range(-radius, radius + 1):
+            s = assembled(buf, dx)
+            for dy in range(NY):
+                put((dx + R) * NY + dy, s[dy])
+
+    def image(op, src, dst, radius):
+        for dx, dy, c in columns(radius):
+            TMP[c] = op(C, src[c], kap_of(dx, dy), sig_of(dx, dy))
+        for dx, dy, c in columns(radius):
+            dst[c] = sz1(C, TMP[c])
+
     def coarse(cyc):
-        Uc = U.at[cyc]
-        def first(dx):
-            s = assembled(Uc, dx)
-            for dy in range(NY):
-                c = (dx + R) * NY + dy
-                d0 = TI * s[dy] * ID1[c]
-                C1B[c] = s[dy]
-                D0B[c] = d0
-                VA[c] = sz1(C, a1(C, d0, kap_of(dx, dy), sig_of(dx, dy)))
-        over(R - 1, first)
-        def second(dx):
-            s = assembled(VA, dx)
-            for dy in range(NY):
-                c = (dx + R) * NY + dy
-                r1 = C1B[c] - s[dy]
-                d1 = ALPHA * D0B[c] + BETA * r1 * ID1[c]
-                t = C("m1") * r1 - a1(C, d1, kap_of(dx, dy), sig_of(dx, dy))
-                R1B[c] = r1
-                D1B[c] = d1
-                VB[c] = sz1(C, restrict2(C, t))
-        over(R - 2, second)
-        def third(dx):
-            s = assembled(VB, dx)
-            for dy in range(NY):
-                c = (dx + R) * NY + dy
-                g0 = TI * s[dy] * ID2[c]
-                C2B[c] = s[dy]
-                G0B[c] = g0
-                VA[c] = sz1(C, a2(C, g0, kap_of(dx, dy), sig_of(dx, dy)))
-        over(R - 3, third)
-        def fourth(dx):
-            s = assembled(VA, dx)
-            for dy in range(NY):
-                c = (dx + R) * NY + dy
-                x2 = (1.0 + ALPHA) * G0B[c] + BETA * (C2B[c] - s[dy]) * ID2[c]
-                q = D1B[c] + prolong2(C, x2)
-                QB[c] = q
-                VC[c] = sz1(C, a1(C, q, kap_of(dx, dy), sig_of(dx, dy)))
-        over(R - 4, fourth)
-        s = assembled(VC, 0)
-        for dy in range(1):
-            c = OWN + dy
-            X1[dy] = D0B[c] + QB[c] + TI * (R1B[c] - s[dy]) * ID1[c]
+        def put1(c, s):
+            C1B[c] = s
+            D0B[c] = TI * s * ID1[c]
+        def put2(c, s):
+            r1 = C1B[c] - s
+            R1B[c] = r1
+            D1B[c] = ALPHA * D0B[c] + BETA * r1 * ID1[c]
+        def put3(c, s):
+            C2B[c] = s
+            G0B[c] = TI * s * ID2[c]
+        def put4(c, s):
+            QB[c] = (1.0 + ALPHA) * G0B[c] + BETA * (C2B[c] - s) * ID2[c]
+        with scope('first'):
+            sums(U.at[cyc], R - 1, put1)
+            image(a1, D0B, VA, R - 1)
+        with scope('second'):
+            sums(VA, R - 2, put2)
+            for dx, dy, c in columns(R - 2):
+                TMP[c] = C("m1") * R1B[c] - a1(C, D1B[c], kap_of(dx, dy), sig_of(dx, dy))
+            for dx, dy, c in columns(R - 2):
+                TMP[c] = yops(C, "r", xops(C, "r", TMP[c]))
+            for dx, dy, c in columns(R - 2):
+                TMP[c] = zops(C, "r", TMP[c])
+            for dx, dy, c in columns(R - 2):
+                VB[c] = sz1(C, TMP[c])
+        with scope('third'):
+            sums(VB, R - 3, put3)
+            image(a2, G0B, VA, R - 3)
+        with scope('fourth'):
+            sums(VA, R - 4, put4)
+            for dx, dy, c in columns(R - 4):
+                TMP[c] = zops(C, "p", QB[c])
+            for dx, dy, c in columns(R - 4):
+                QB[c] = D1B[c] + xops(C, "p", yops(C, "p", TMP[c]))
+            image(a1, QB, VC, R - 4)
+        with scope('fifth'):
+            def put5(c, s):
+                X1[c] = D0B[c] + QB[c] + TI * (R1B[c] - s) * ID1[c]
+            sums(VC, R - 5, put5)
 
     def restrict1(t):
         xs = [sum(float(J1[i, a]) * t[i] for i in range(8)) for a in range(4)]
@@ -456,19 +508,67 @@
                     out = p if out is None else out + p
         return out
 
-    def prolong1(e):
-        z = [None, None]
-        for d in PZ:
-            r = lr(e, d) if d else e
-            for hh in PZ[d]:
-                p = C(f"pz{hh}_{d}") * r
-                z[hh] = p if z[hh] is None else z[hh] + p
-        V[0:8] = z[0]
-        V[8:16] = z[1]
-        ex = []
-        for a in range(4):
-            ex.append(sum(C(f"py{bb}") * V[pl.ds((bb % 2) * 8 + 2 * a + bb // 2, 8, stride=0)] for bb in range(4)))
-        return [sum(float(J1[i, a]) * ex[a] for a in range(4)) for i in range(8)]
+    around = [(dx, dy) for dx in (-1, 0, 1) for dy in (-1, 0, 1)]
+
+    def lines():
+        for n, (dx, dy) in enumerate(around):
+            e = X1[slot(dx, dy)]
+            z = [None] * 4
+            for d in range(-7, 8):
+                r = lr(e, d) if d else e
+                for hh in range(2):
+                    for q, tag in enumerate(("pz", "qz")):
+                        if not live(f"{tag}{hh}_{d}"):
+                            continue
+                        p = C(f"{tag}{hh}_{d}") * r
+                        z[2 * q + hh] = p if z[2 * q + hh] is None else z[2 * q + hh] + p
+            for q in range(4):
+                Z[n, 8 * q:8 * q + 8] = z[q]
+
+    def line(n, q, a, b):
+        return Z[n, pl.ds(16 * q + 8 * (b % 2) + 2 * a + b // 2, 8, stride=0)]
+
+    def planes(n, a):
+        return sum(C(f"py{b}") * line(n, 0, a, b) for b in range(4))
+
+    def planes_image(n, a, rho_n, ex):
+        return sum(C(f"qy{b}") * line(n, 0, a, b) + C(f"py{b}") * line(n, 1, a, b) for b in range(4)) + rho_n * ex
+
+    def correction():
+        lines()
+        rhos = [row(dx, dy, 1) / row(dx, dy, 0) for dx, dy in around]
+        ex = [planes(4, a) for a in range(4)]
+        ey = [planes_image(4, a, rho, ex[a]) for a in range(4)]
+        e = [sum(float(J1[i, a]) * ex[a] for a in range(4)) for i in range(8)]
+        for i in range(8):
+            V[8 * i:8 * i + 8] = c1 * (sum(float(KJx[i, a]) * ex[a] for a in range(4)) + w8[i] * sum(float(J1[i, a]) * ey[a] for a in range(4)))
+        for n, (dx, dy) in enumerate(around):
+            kap_n, rho_n = row(dx, dy, 0), rhos[n]
+            i0, j0 = (7 if dx < 0 else 0), (7 if dy < 0 else 0)
+            a0, b0 = (3 if dx < 0 else 0), (3 if dy < 0 else 0)
+            if dx and dy:
+                t = C(f"fc{i0}{j0}_0") * Z[n, 0:8] + C(f"fc{i0}{j0}_1") * Z[n, 8:16]
+                hh = b0 % 2
+                t = t + C(f"fo{i0}{j0}") * (Z[n, 16 + 8 * hh:24 + 8 * hh] + rho_n * Z[n, 8 * hh:8 * hh + 8])
+                t = t + sr(t, 4)
+                t = t + sr(t, 2)
+                t = t + sr(t, 1)
+                r = 8 * (7 - i0) + 7 - j0
+                V[r:r + 1] = V[r:r + 1] + (kap_n * (w8[i0] * C("wyz")[0:1] * (w8[j0] / w8[0]))) * t[0:1]
+            elif dx:
+                q = [planes(n, a) for a in range(4)]
+                t = sum(float(KJx[i0, a]) * q[a] for a in range(4)) + w8[i0] * planes_image(n, a0, rho_n, q[a0])
+                r = 8 * (7 - i0)
+                V[r:r + 8] = V[r:r + 8] + (kap_n * C("wyz")) * t
+            elif dy:
+                t = C(f"fy{j0}_0") * Z[n, 0:8] + C(f"fy{j0}_1") * Z[n, 8:16]
+                t = t + jnp.where(halves()[0], sr(t, 1), sr(t, -1))
+                hh = b0 % 2
+                t = t + Z[n, 16 + 8 * hh:24 + 8 * hh] + rho_n * Z[n, 8 * hh:8 * hh + 8]
+                Z[n, 32:40] = t
+                f = sum(C(f"py{a}") * Z[n, pl.ds(32 + 2 * a + b0 // 2, 8, stride=0)] + C(f"qy{a}") * line(n, 0, a, b0) for a in range(4))
+                V[pl.ds(7 - j0, 8, stride=8)] = V[pl.ds(7 - j0, 8, stride=8)] + (kap_n * C("wyz") * w8[j0]) * f
+        return e
 
     def apply(rnd, v):
         face_start(rnd, [sz8(C, t) for t in a_fine(C, v, c1, rho)])
@@ -492,20 +592,27 @@
         u = sz1(C, restrict1(t))
         us[cyc] = u
         U[cyc, OWN] = u
-        for dx, dy in PARTNERS:
-            u_copy(cyc, dx, dy).start()
+        with scope('u_send'):
+            for dx, dy in PARTNERS:
+                u_copy(cyc, dx, dy).start()
+        face_start(rnd + 1, [sz8(C, p) for p in w])
         @pl.when(cyc == 0)
         def _():
+            coarse_diagonals()
             pl.semaphore_wait(chain.at[1], 2)
             for k in (-10, 10):
                 pl.semaphore_signal(chain.at[2], inc=1, device_id=zring(k), device_id_type=MESH)
-        all_but_one(U.at[cyc], u_send.at[cyc], u_recv.at[cyc]).wait_recv()
+        s = face_wait(rnd + 1)
+        for i in range(8):
+            R1[i] = R1[i] - s[i]
+        with scope('u_wait'):
+            landed(U.at[cyc], NC - 1, u_send.at[cyc], u_recv.at[cyc]).wait_recv()
         coarse(cyc)
-        e = prolong1(X1[0])
-        q = [Q[i] + e[i] for i in range(8)]
+        with scope('corr'):
+            e = correction()
         for i in range(8):
-            Q[i] = q[i]
-        s = apply(rnd + 1, q)
+            Q[i] = Q[i] + e[i]
+        s = [sz8(C, V[8 * i:8 * i + 8]) for i in range(8)]
         dl = []
         for i in range(8):
             r3 = R1[i] - s[i]
@@ -531,14 +638,19 @@
     pl.semaphore_wait(chain.at[3], 3)
     def z_copy(k):
         return pltpu.make_async_remote_copy(src_ref=ap, dst_ref=AZ.at[zc], send_sem=z_send, recv_sem=z_recv, device_id=zring(k), device_id_type=MESH)
-    for k in range(1, ZR // 2):
-        z_copy(k).start()
-        z_copy(-k).start()
-    z_copy(ZR // 2).start()
+    with scope('z_send'):
+        for k in range(1, ZR // 2):
+            z_copy(k).start()
+            z_copy(-k).start()
+        z_copy(ZR // 2).start()
+    stores = [pltpu.make_async_copy(a, b, out_sem.at[k]) for k, (a, b) in enumerate(((XS, z_out), (B, b_out), (R1, r_out)))]
+    for c in stores:
+        c.start()
     def most(buf, send, recv):
         return pltpu.make_async_remote_copy(src_ref=buf.at[pl.ds(0, 31)], dst_ref=buf.at[pl.ds(0, 31)], send_sem=send, recv_sem=recv,
                                             device_id=at(1, 0), device_id_type=MESH)
-    most(AZ, z_send, z_recv).wait_recv()
+    with scope('z_wait'):
+        most(AZ, z_send, z_recv).wait_recv()
     part = AZ[0]
     for k in range(1, ZR):
         part = part + AZ[k]
@@ -550,23 +662,26 @@
         return pltpu.make_async_remote_copy(src_ref=pp, dst_ref=AP.at[pi], send_sem=p_send, recv_sem=p_recv, device_id=plane(*o), device_id_type=MESH)
     for o in others:
         p_copy(o).start()
-    most(AP, p_send, p_recv).wait_recv()
+    with scope('p_wait'):
+        most(AP, p_send, p_recv).wait_recv()
     tot = AP[0]
     for k in range(1, 32):
         tot = tot + AP[k]
     bb, br, rr = tot[0:1, 0:1], tot[0:1, 1:2], tot[0:1, 2:3]
     ww = bb - 2.0 * br + rr
     coef = (bb - br) / ww
-    for i in range(8):
-        sol[i] = coef * XS[i]
-        res[i] = B[i] - coef * (B[i] - R1[i])
-    rel[...] = jnp.broadcast_to(jnp.sqrt((bb * rr - br * br) / (ww * bb)), (1, 128))
-
-    most(AP, p_send, p_recv).wait_send()
+    size = jnp.sqrt((bb * rr - br * br) / (ww * bb))
+    scal[...] = jnp.where(ln == 0, coef, size)
+    for c in stores:
+        c.wait()
+
+    with scope('send_waits'):
+        most(AP, p_send, p_recv).wait_send()
     most(AZ, z_send, z_recv).wait_send()
-    all_but_one(KS, ks_send, ks_recv).wait_send()
+    landed(KS, len(near), ks_send, ks_recv).wait_send()
+    landed(KS, len(far), kf_send, kf_recv).wait_send()
     for cyc in range(2):
-        all_but_one(U.at[cyc], u_send.at[cyc], u_recv.at[cyc]).wait_send()
+        landed(U.at[cyc], NC - 1, u_send.at[cyc], u_recv.at[cyc]).wait_send()
     for rnd in range(ROUNDS):
         for c in face_copies(rnd):
             c.wait_send()
@@ -581,35 +696,35 @@
     fine = pltpu.VMEM((8, 8, 128), f32)
     row = pltpu.VMEM((1, 128), f32)
     scratch = [
-        pltpu.VMEM((len(NAMES), 8, 128), f32), pltpu.VMEM((64, 128), f32),
+        pltpu.VMEM((len(NAMES), 8, 128), f32), fine, pltpu.VMEM((1, 16), f32), pltpu.VMEM((1, 16), f32), pltpu.VMEM((64, 128), f32),
         pltpu.VMEM((2, 128), f32), pltpu.VMEM((NC, 2, 128), f32),
         pltpu.VMEM((ROUNDS, 2, 8, 128), f32), pltpu.VMEM((ROUNDS, 2, 8, 128), f32), pltpu.VMEM((ROUNDS, 4, 1, 128), f32),
         pltpu.VMEM((ROUNDS, 2, 8, 128), f32), pltpu.VMEM((ROUNDS, 2, 8, 128), f32), pltpu.VMEM((ROUNDS, 4, 1, 128), f32),
         fine, fine, fine, fine, fine, fine,
         pltpu.VMEM((2, 8, 128), f32), pltpu.VMEM((2, NC, 8, 128), f32),
-        col, col, col, col, col, col, col, col, col, col, col, col, pltpu.VMEM((NY, 8, 128), f32),
+        col, col, col, col, col, col, col, col, col, col, col, col, col, col, pltpu.VMEM((9, 40, 128), f32),
         row, pltpu.VMEM((32, 1, 128), f32), row, pltpu.VMEM((32, 1, 128), f32),
-        pltpu.SemaphoreType.DMA, pltpu.SemaphoreType.DMA, pltpu.SemaphoreType.DMA,
+        pltpu.SemaphoreType.DMA((4,)), pltpu.SemaphoreType.DMA((3,)),
+        pltpu.SemaphoreType.DMA, pltpu.SemaphoreType.DMA, pltpu.SemaphoreType.DMA, pltpu.SemaphoreType.DMA,
         pltpu.SemaphoreType.DMA((ROUNDS, 8)), pltpu.SemaphoreType.DMA((ROUNDS, 8)),
         pltpu.SemaphoreType.DMA((2,)), pltpu.SemaphoreType.DMA((2,)),
         pltpu.SemaphoreType.DMA, pltpu.SemaphoreType.DMA, pltpu.SemaphoreType.DMA, pltpu.SemaphoreType.DMA,
         pltpu.SemaphoreType.REGULAR((4,)),
     ]
-    vm = pl.BlockSpec(memory_space=pltpu.VMEM)
+    hbm = pl.BlockSpec(memory_space=pl.ANY)
     call = pl.pallas_call(
         kernel,
-        out_shape=[jax.ShapeDtypeStruct((8, 8, 128), f32), jax.ShapeDtypeStruct((8, 8, 128), f32), jax.ShapeDtypeStruct((1, 128), f32)],
-        in_specs=[pl.BlockSpec(memory_space=pl.ANY), vm, vm, vm, vm],
-        out_specs=[vm, vm, vm],
+        out_shape=[jax.ShapeDtypeStruct((8, 8, 128), f32)] * 3 + [jax.ShapeDtypeStruct((1, 128), f32)],
+        in_specs=[hbm] * 4,
+        out_specs=[hbm] * 3 + [pl.BlockSpec(memory_space=pltpu.VMEM)],
         scratch_shapes=scratch,
         compiler_params=pltpu.CompilerParams(collective_id=0, has_side_effects=True),
         name="helmholtz",
     )
-    hot = (np.arange(128)[None, :] // 8 == np.arange(16)[:, None]).astype(np.float32)
-
     def local(forcing, kappa, sigma):
-        s, r, e = call(jnp.asarray(TABLE), forcing, kappa.reshape(1, 16), sigma.reshape(1, 16), jnp.asarray(hot))
-        return s, r, e[0, 0]
+        z, b, r, scal = call(jnp.asarray(TABLE), forcing, kappa.reshape(1, 16), sigma.reshape(1, 16))
+        coef = scal[0, 0]
+        return coef * z, b - coef * (b - r), scal[0, 1]
 
     return jax.shard_map(local, mesh=mesh, in_specs=(P("gx", "gy", None),) * 3,
                          out_specs=(P("gx", "gy", None), P("gx", "gy", None), P()), check_vma=False)

time: 109 us -> 87.6 us (0.80)
  Pallas kernels: 105 us -> 83.4 us
  other arithmetic: 0 us -> 2.05 us
  between operations: 1.81 us -> 0.65 us
    pallas_call x1, Pallas kernels: 105 us -> 83.4 us  [local(): call(jnp.asarray(TABLE), forcing, kappa.reshape(1, 16), sigma.reshape(1,...]
    sub x0 -> x1, other arithmetic: none -> 2.05 us  [local(): return (coef * z, b - coef * (b - r), scal[0, 1])]
    unnamed x6 -> x2, local copies, waits for them, and re-layouts: 2.06 us -> 0.65 us
where the time goes in v2:
time: 87.6 us; the launch traced here: 87.3 us
  Pallas kernels  83.4 us (95%)
  other arithmetic  2.05 us (2%)
  local copies, waits for them, and re-layouts  1.23 us (1%)
    pallas_call x1, Pallas kernels, local(): call(jnp.asarray(TABLE), forcing, kappa.reshape(1, 16), sigma.reshape(1,...  83.4 us
    sub x1, other arithmetic, local(): return (coef * z, b - coef * (b - r), scal[0, 1])  2.05 us

profile of v2, /device:TPU:1, one launch (start us, length us, event | category | flops | bytes accessed | tf_op | source)
XLA Modules:
  0.0 87.3 jit_solution(2202154047731953712)
XLA Ops:
  0.6 83.4 %helmholtz.1 = (f32[8,8,128]{2,1,0:T(8,128)}, f32[8,8,128]{2,1,0:T(8,128)}, f32[8,8,128]{2,1,0:T(8,128)}, f32[1,128]{1,0:T(1,128)}) custom-call(f32[212,8,128]{2,1,0:T(8,128)} %constant.2.clone.tab_hbm, f32[8,8,128]{2,1,0:T(8,128)} %forc_hbm.1, f32[1,16]{1,0:T(1,128)} %bitcast.4, f32[1,16]{1,0:T(1,128)} %bitcast.5), custom_call_target="tpu_custom_call" | custom-call | tf_op jit(solution)/shard_map/helmholtz/pallas_call | solution.py:725
  84.0 0.0 copy-start
  84.0 0.6 copy-done
  84.7 0.6 fusion
  85.3 2.1 %multiply_subtract_fusion = (f32[8,8,128]{2,1,0:T(8,128)}, f32[8,8,128]{2,1,0:T(8,128)}) fusion(f32[8,8,128]{2,1,0:T(8,128)} %get-tuple-element.9, f32[8,8,128]{2,1,0:T(8,128)} %get-tuple-element.10, f32[]{:T(128)} %bitcast.2, f32[8,8,128]{2,1,0:T(8,128)} %get-tuple-element.8), kind=kLoop, calls=%fused_computation | loop fusion | flops 32768 | bytes 163844 | tf_op jit(solution)/shard_map/sub | solution.py:727
Async XLA Ops:
  84.0 0.7 copy-start

commit v3 on v2

--- a/solution.py
+++ b/solution.py
@@ -67,10 +67,10 @@
     put(f"gk{i}", (Kd8[i] * w8[sub] + w8[i] * Kd8[sub]) * w8[kz] + w8[i] * w8[sub] * Kd8[kz])
     put(f"gw{i}", w8[i] * w8[sub] * w8[kz])
 put("m8", f8[sub] * f8[kz])
-i4 = sub // 2; jp = sub % 2; h = lane % 2; k4 = (lane % 8) // 2; j4 = 2 * jp + h
+i4 = sub // 2; jp = sub % 2; h = lane % 2; k4 = (lane % 8) // 2; j4 = 2 * jp + (h ^ jp); jsw = 2 * (1 - jp) + (h ^ (1 - jp)); jot = 2 * jp + ((1 - h) ^ jp)
 for j in range(8):
     for hh in range(2):
-        put(f"ry{j}_{hh}", J1[j, 2 * jp + hh] * ones)
+        put(f"ry{j}_{hh}", J1[j, 2 * jp + (hh ^ jp)] * ones)
 RZ = []
 for hh in range(2):
     for d in range(-7, 8):
@@ -89,8 +89,8 @@
     if "x" in dirs:
         for d in range(4): put(f"{tag}x{d}", M[i4, (i4 - d) % 4] * ones)
     if "y" in dirs:
-        put(f"{tag}ya", M[j4, j4]); put(f"{tag}yb", M[j4, 2 * (1 - jp) + h])
-        put(f"{tag}yc", M[2 * jp + 1 - h, j4]); put(f"{tag}yd", M[2 * jp + 1 - h, 2 * (1 - jp) + h])
+        put(f"{tag}ya", M[j4, j4]); put(f"{tag}yb", M[j4, jsw])
+        put(f"{tag}yc", M[jot, j4]); put(f"{tag}yd", M[jot, jsw])
     if "z" in dirs:
         for d in range(-3, 4):
             src = k4 - d; ok = (src >= 0) & (src < 4)
@@ -124,12 +124,12 @@
         put(f"qz{hh}_{d}", np.where(ok, KJ[kz, np.clip(src // 2, 0, 3)], 0.0))
 for b in range(4): put(f"qy{b}", KJ[sub, b] * ones)
 for j0 in (0, 7):
-    for hh in range(2): put(f"fy{j0}_{hh}", KJ[j0, 2 * jp + hh] * ones)
+    for hh in range(2): put(f"fy{j0}_{hh}", KJ[j0, 2 * jp + (hh ^ jp)] * ones)
 for i0 in (0, 7):
     for j0 in (0, 7):
         a0, b0 = (0 if i0 == 0 else 3), (0 if j0 == 0 else 3)
         for hh in range(2):
-            b_ = 2 * jp + hh
+            b_ = 2 * jp + (hh ^ jp)
             put(f"fc{i0}{j0}_{hh}", (KJ[i0, i4] * (b_ == b0) + KJ[j0, b_] * (i4 == a0)) * ones)
         put(f"fo{i0}{j0}", ((i4 == a0) & (jp == b0 // 2)) * ones)
 for q in range(2): put(f"hot{q}", (lane // 8 == sub + 8 * q) * 1.0)
@@ -207,21 +207,26 @@
 def sz1(C, v): return v + C("z0") * lr(v, 2) + C("z3") * lr(v, -2)
 def xfrom_l(C, v): return C("x0") * sr(v, 2)
 def xfrom_r(C, v): return C("x3") * sr(v, -2)
-def yfrom_l(C, v): return C("y0") * lr(sr(v, -1), -1)
-def yfrom_r(C, v): return C("y3") * lr(sr(v, 1), 1)
-
-def a_fine(C, v, c1, rho):
-    e = C("cyz0") + rho
-    out = []
+def yfrom_l(C, v): return C("y0") * sr(v, -1)
+def yfrom_r(C, v): return C("y3") * sr(v, 1)
+
+def a_fine(C, v, kap, sig, sides):
+    kap_y, kap_x, sig_x = sides
+    out, to_x, to_y = [], [], []
     for i in range(8):
-        t = e * v[i]
+        t = C("cyz0") * v[i]
         for d in range(1, 8): t = t + C(f"cy{d}") * sr(v[i], d)
         for d in range(-7, 8):
             if d: t = t + C(f"cz{d}") * lr(v[i], d)
         x = K8[i][0] * v[0]
         for a in range(1, 8): x = x + K8[i][a] * v[a]
-        out.append(c1 * (x + w8[i] * t))
-    return out
+        o = C("wyz") * (kap * (x + w8[i] * t) + sig * (w8[i] * v[i]))
+        out.append(o)
+        if i in (0, 7):
+            s = i // 7
+            to_x.append(o + C("wyz") * (kap_y * x))
+            to_y.append(o + C("wyz") * (w8[i] * (kap_x[s] * t + sig_x[s] * v[i])))
+    return out, to_x, to_y
 
 def sz8(C, v): return v + C("mz0") * lr(v, 1) + C("mz7") * lr(v, -1)
 
@@ -238,20 +243,24 @@
 R = 6
 NC = (2 * R + 1) * NY
 OWN = R * NY
-PARTNERS = [(dx, dy) for dx in range(-R, R + 1) for dy in range(NY) if (dx, dy) != (0, 0)]
+PARTNERS = [(dx, dy) for far in range(R, -1, -1) for dy in (2, 1, 3, 0) for dx in ((-far, far) if far else (0,)) if (dx, dy) != (0, 0)]
 ROUNDS = 7
 TI = 1.0 / THETA
+NEAR = 3
+EDGE = (-R, R)
+EDGE_ROWS = {R: (6, 2), -R: (0, 2)}
+U_TILES = NC - 1 - 2 * NY + 2 * NY // 4
 
 
 def slot(dx, dy):
     return (dx + R) * NY + dy % NY
 
 
-def kernel(tab_hbm, forc_hbm, kap_hbm, sig_hbm, z_out, b_out, r_out, scal,
-           tab, forc, kap_in, sig_in, V, ks_s, KS, SX, SY, SC, RX, RY, RC, ID0, B, D0, R1, Q, XS,
+def kernel(tab_hbm, forc_hbm, kap_hbm, sig_hbm, XS, B, R1, coef_out, rel_out,
+           tab, forc, kap_in, sig_in, V, ks_s, KS, FS, SC, FR, RC, ID0, D0, Q,
            us, U, ID1, ID2, C1B, D0B, VA, R1B, D1B, VB, C2B, G0B, QB, VC, X1, TMP, Z,
            ap, AZ, pp, AP,
-           in_sem, out_sem, ks_send, kf_send, kf_recv, ks_recv, f_send, f_recv, u_send, u_recv,
+           in_sem, ks_send, kf_send, kf_recv, ks_recv, c_send, c_recv, f_send, f_recv, u_send, u_recv,
            z_send, z_recv, p_send, p_recv, chain):
     gx = lax.axis_index("gx")
     gy = lax.axis_index("gy")
@@ -259,8 +268,11 @@
     zc = lax.rem(gx // 2, ZR)
     yc = gx // (2 * ZR)
 
+    gxs = {dx: lax.rem(gx + dx + GX, GX) for dx in range(-R, R + 1)}
+    gys = [lax.rem(gy + dy, NY) for dy in range(NY)]
+
     def at(dx, dy):
-        return (lax.rem(gx + dx + GX, GX), lax.rem(gy + dy + NY, NY))
+        return (gxs[dx], gys[dy % NY])
 
     def zring(k):
         return (yc * (2 * ZR) + 2 * lax.rem(zc + k + ZR, ZR) + core, gy)
@@ -274,9 +286,13 @@
     loads = [pltpu.make_async_copy(a, b, in_sem.at[k]) for k, (a, b) in enumerate(((kap_hbm, kap_in), (sig_hbm, sig_in), (tab_hbm, tab), (forc_hbm, forc)))]
     for c in loads:
         c.start()
+    for cyc in range(2):
+        for dx in EDGE:
+            for dy in range(NY):
+                U[cyc, slot(dx, dy)] = jnp.zeros((8, 128), jnp.float32)
     barrier = pltpu.get_barrier_semaphore()
-    greet = [at(dx, dy) for dx, dy in PARTNERS]
-    greet += [zring(k) for k in (-3, -2, -1, 1, 2, 3)] + [plane(k, 0, 0) for k in (1, 2, 3)]
+    greet = [at(dx, dy) for dx, dy in PARTNERS if abs(dx) <= NEAR]
+    greet += [zring(-1), zring(1), plane(1, 0, 0), plane(3, 0, 0)]
     for d in greet:
         pl.semaphore_signal(barrier, inc=1, device_id=d, device_id_type=MESH)
 
@@ -293,47 +309,45 @@
     KS[OWN, 0:1] = kap[0:1]
     KS[OWN, 1:2] = sig[0:1]
 
-    def put_faces(rnd):
-        SX[rnd, 0] = V[0:8]
-        SX[rnd, 1] = V[56:64]
-        SY[rnd, 0] = V[pl.ds(0, 8, stride=8)]
-        SY[rnd, 1] = V[pl.ds(7, 8, stride=8)]
-        for k, row in enumerate((0, 7, 56, 63)):
-            SC[rnd, k] = V[row:row + 1]
-
-    def face_copies(rnd):
-        out = []
-        for s in range(2):
-            step = 2 * s - 1
-            out.append((SX.at[rnd, s], RX.at[rnd, 1 - s], at(step, 0)))
-        for s in range(2):
-            step = 2 * s - 1
-            out.append((SY.at[rnd, s], RY.at[rnd, 1 - s], at(0, step)))
-        for k in range(4):
-            out.append((SC.at[rnd, k], RC.at[rnd, 3 - k], at(2 * (k // 2) - 1, 2 * (k % 2) - 1)))
-        return [pltpu.make_async_remote_copy(src_ref=a, dst_ref=b, send_sem=f_send.at[rnd, n], recv_sem=f_recv.at[rnd, RSEM[n]],
-                                             device_id=d, device_id_type=MESH) for n, (a, b, d) in enumerate(out)]
-
-    def face_start(rnd, tiles):
+    def side_copies(rnd):
+        to = [at(-1, 0), at(1, 0), at(0, -1), at(0, 1)]
+        return [pltpu.make_async_remote_copy(src_ref=FS.at[rnd, n], dst_ref=FR.at[rnd, n ^ 1], send_sem=f_send, recv_sem=f_recv.at[rnd],
+                                             device_id=d, device_id_type=MESH) for n, d in enumerate(to)]
+
+    def corner_copies():
+        return [pltpu.make_async_remote_copy(src_ref=SC.at[k], dst_ref=RC.at[3 - k], send_sem=c_send, recv_sem=c_recv,
+                                             device_id=at(2 * (k // 2) - 1, 2 * (k % 2) - 1), device_id_type=MESH) for k in range(4)]
+
+    def whole(buf, send, recv):
+        return pltpu.make_async_remote_copy(src_ref=buf, dst_ref=buf, send_sem=send, recv_sem=recv, device_id=at(1, 0), device_id_type=MESH)
+
+    def keep(tiles):
         for i in range(8):
             V[8 * i:8 * i + 8] = tiles[i]
-        put_faces(rnd)
+
+    def face_start(rnd, to_x, to_y):
+        for s in range(2):
+            FS[rnd, s] = to_x[s]
+            FS[rnd, 2 + s] = V[pl.ds(7 * s, 8, stride=8)]
+            if to_y is not None:
+                FS[rnd, 2 + s, 0:1] = to_y[0][7 * s:7 * s + 1]
+                FS[rnd, 2 + s, 7:8] = to_y[1][7 * s:7 * s + 1]
         with scope('face_start'):
-            for c in face_copies(rnd):
+            for c in side_copies(rnd):
                 c.start()
 
-    def face_wait(rnd):
+    def face_wait(rnd, corners=False):
         with scope('face_wait'):
-            for n in range(8):
-                pltpu.make_async_remote_copy(src_ref=(RX.at[rnd, n] if n < 2 else RY.at[rnd, n - 2] if n < 4 else RC.at[rnd, n - 4]),
-                                             dst_ref=(RX.at[rnd, n] if n < 2 else RY.at[rnd, n - 2] if n < 4 else RC.at[rnd, n - 4]),
-                                             send_sem=f_send.at[rnd, n], recv_sem=f_recv.at[rnd, n], device_id=at(1, 0), device_id_type=MESH).wait_recv()
-        V[0:8] = V[0:8] + RX[rnd, 0]
-        V[56:64] = V[56:64] + RX[rnd, 1]
-        V[pl.ds(0, 8, stride=8)] = V[pl.ds(0, 8, stride=8)] + RY[rnd, 0]
-        V[pl.ds(7, 8, stride=8)] = V[pl.ds(7, 8, stride=8)] + RY[rnd, 1]
-        for k, row in enumerate((0, 7, 56, 63)):
-            V[row:row + 1] = V[row:row + 1] + RC[rnd, k]
+            whole(FR.at[rnd], f_send, f_recv.at[rnd]).wait_recv()
+            if corners:
+                whole(RC, c_send, c_recv).wait_recv()
+        V[0:8] = V[0:8] + FR[rnd, 0]
+        V[56:64] = V[56:64] + FR[rnd, 1]
+        for s in range(2):
+            V[pl.ds(7 * s, 8, stride=8)] = V[pl.ds(7 * s, 8, stride=8)] + FR[rnd, 2 + s]
+        if corners:
+            for k, r in enumerate((0, 7, 56, 63)):
+                V[r:r + 1] = V[r:r + 1] + RC[k]
         return [V[8 * i:8 * i + 8] for i in range(8)]
 
     first_v = [sz8(C, forc[i]) for i in range(8)]
@@ -348,14 +362,22 @@
     far = [p for p in PARTNERS if p not in near]
     for p in near:
         ks_copy(*p).start()
-    face_start(0, first_v)
-    with scope('ks_send'):
-        for p in far:
-            ks_copy(*p).start()
-    for k in (-3, 3):
-        pl.semaphore_signal(chain.at[0], inc=1, device_id=zring(k), device_id_type=MESH)
-    for k in (1, 2, 3):
-        pl.semaphore_signal(chain.at[3], inc=1, device_id=plane(k, 0, 0), device_id_type=MESH)
+    keep(first_v)
+    for k, r in enumerate((0, 7, 56, 63)):
+        SC[k] = V[r:r + 1]
+    for c in corner_copies():
+        c.start()
+    face_start(0, (first_v[0], first_v[7]), None)
+    def tell(n, to):
+        for d in to:
+            pl.semaphore_signal(chain.at[n], inc=1, device_id=d, device_id_type=MESH)
+
+    def told(n, count=2):
+        pl.semaphore_wait(chain.at[n], count)
+
+    tell(0, (at(-NEAR, 0), at(NEAR, 0)))
+    tell(1, (zring(-1), zring(1)))
+    tell(5, (plane(1, 0, 0), plane(3, 0, 0)))
 
     def landed(buf, count, send, recv):
         return pltpu.make_async_remote_copy(src_ref=buf.at[pl.ds(0, count)], dst_ref=buf.at[pl.ds(0, count)], send_sem=send, recv_sem=recv,
@@ -379,7 +401,15 @@
         ii = min(i, 7 - i)
         ID0[i] = 1.0 / sz8(C, kk * C(f"gk{ii}") + ss * C(f"gw{ii}"))
 
-    b = face_wait(0)
+    b = face_wait(0, True)
+    told(0)
+    with scope('ks_send'):
+        for p in far:
+            ks_copy(*p).start()
+    told(1)
+    tell(2, (zring(-2), zring(2)))
+    told(5)
+    tell(6, (plane(2, 0, 0),))
     for i in range(8):
         B[i] = b[i]
         R1[i] = b[i]
@@ -421,9 +451,7 @@
         with scope('g_two'):
             over(R - 1, g_two)
 
-    pl.semaphore_wait(chain.at[0], 2)
-    for k in (-6, 6):
-        pl.semaphore_signal(chain.at[1], inc=1, device_id=zring(k), device_id_type=MESH)
+    sides = (C("jm0") * row(0, -1, 0) + C("jm7") * row(0, 1, 0), (row(-1, 0, 0), row(1, 0, 0)), (row(-1, 0, 1), row(1, 0, 1)))
 
     c1 = kap * C("wyz")
     rho = sig / kap
@@ -432,7 +460,8 @@
         return [ref[i] for i in range(8)]
 
     def u_copy(cyc, dx, dy):
-        return pltpu.make_async_remote_copy(src_ref=us.at[cyc], dst_ref=U.at[cyc, slot(-dx, -dy)], send_sem=u_send.at[cyc], recv_sem=u_recv.at[cyc],
+        rows = pl.ds(*EDGE_ROWS[dx]) if dx in EDGE_ROWS else slice(None)
+        return pltpu.make_async_remote_copy(src_ref=us.at[cyc, rows], dst_ref=U.at[cyc, slot(-dx, -dy), rows], send_sem=u_send, recv_sem=u_recv.at[cyc],
                                             device_id=at(dx, dy), device_id_type=MESH)
 
     def columns(radius):
@@ -526,7 +555,7 @@
                 Z[n, 8 * q:8 * q + 8] = z[q]
 
     def line(n, q, a, b):
-        return Z[n, pl.ds(16 * q + 8 * (b % 2) + 2 * a + b // 2, 8, stride=0)]
+        return Z[n, pl.ds(16 * q + 8 * ((b % 2) ^ (b // 2)) + 2 * a + b // 2, 8, stride=0)]
 
     def planes(n, a):
         return sum(C(f"py{b}") * line(n, 0, a, b) for b in range(4))
@@ -548,8 +577,7 @@
             a0, b0 = (3 if dx < 0 else 0), (3 if dy < 0 else 0)
             if dx and dy:
                 t = C(f"fc{i0}{j0}_0") * Z[n, 0:8] + C(f"fc{i0}{j0}_1") * Z[n, 8:16]
-                hh = b0 % 2
-                t = t + C(f"fo{i0}{j0}") * (Z[n, 16 + 8 * hh:24 + 8 * hh] + rho_n * Z[n, 8 * hh:8 * hh + 8])
+                t = t + C(f"fo{i0}{j0}") * (Z[n, 16:24] + rho_n * Z[n, 0:8])
                 t = t + sr(t, 4)
                 t = t + sr(t, 2)
                 t = t + sr(t, 1)
@@ -563,15 +591,20 @@
             elif dy:
                 t = C(f"fy{j0}_0") * Z[n, 0:8] + C(f"fy{j0}_1") * Z[n, 8:16]
                 t = t + jnp.where(halves()[0], sr(t, 1), sr(t, -1))
-                hh = b0 % 2
-                t = t + Z[n, 16 + 8 * hh:24 + 8 * hh] + rho_n * Z[n, 8 * hh:8 * hh + 8]
+                t = t + Z[n, 16:24] + rho_n * Z[n, 0:8]
                 Z[n, 32:40] = t
                 f = sum(C(f"py{a}") * Z[n, pl.ds(32 + 2 * a + b0 // 2, 8, stride=0)] + C(f"qy{a}") * line(n, 0, a, b0) for a in range(4))
                 V[pl.ds(7 - j0, 8, stride=8)] = V[pl.ds(7 - j0, 8, stride=8)] + (kap_n * C("wyz") * w8[j0]) * f
         return e
 
+    def image_start(rnd, v):
+        out, to_x, to_y = a_fine(C, v, kap, sig, sides)
+        keep([sz8(C, t) for t in out])
+        face_start(rnd, [sz8(C, t) for t in to_x], [sz8(C, t) for t in to_y])
+        return out
+
     def apply(rnd, v):
-        face_start(rnd, [sz8(C, t) for t in a_fine(C, v, c1, rho)])
+        image_start(rnd, v)
         return face_wait(rnd)
 
     def cycle(cyc, carry):
@@ -587,7 +620,7 @@
             R1[i] = r1
             d1.append(ALPHA * D0[i] + BETA * r1 * ID0[i])
             Q[i] = d1[i]
-        w = a_fine(C, d1, c1, rho)
+        w, to_x, to_y = a_fine(C, d1, kap, sig, sides)
         t = [float(f8[i]) * C("m8") * R1[i] - w[i] for i in range(8)]
         u = sz1(C, restrict1(t))
         us[cyc] = u
@@ -595,19 +628,24 @@
         with scope('u_send'):
             for dx, dy in PARTNERS:
                 u_copy(cyc, dx, dy).start()
-        face_start(rnd + 1, [sz8(C, p) for p in w])
+        keep([sz8(C, p) for p in w])
+        face_start(rnd + 1, [sz8(C, p) for p in to_x], [sz8(C, p) for p in to_y])
         @pl.when(cyc == 0)
         def _():
             coarse_diagonals()
-            pl.semaphore_wait(chain.at[1], 2)
-            for k in (-10, 10):
-                pl.semaphore_signal(chain.at[2], inc=1, device_id=zring(k), device_id_type=MESH)
+            told(2)
+            tell(3, (zring(-4), zring(4)))
+            told(6, 1)
         s = face_wait(rnd + 1)
         for i in range(8):
             R1[i] = R1[i] - s[i]
         with scope('u_wait'):
-            landed(U.at[cyc], NC - 1, u_send.at[cyc], u_recv.at[cyc]).wait_recv()
+            landed(U.at[cyc], U_TILES, u_send, u_recv.at[cyc]).wait_recv()
         coarse(cyc)
+        @pl.when(cyc == 0)
+        def _():
+            told(3)
+            tell(4, (zring(-8), zring(8)))
         with scope('corr'):
             e = correction()
         for i in range(8):
@@ -634,8 +672,7 @@
     mine = jnp.where(ln == 0, dot(B, B), jnp.where(ln == 1, dot(B, R1), dot(R1, R1)))
     ap[...] = mine
     AZ[zc] = mine
-    pl.semaphore_wait(chain.at[2], 2)
-    pl.semaphore_wait(chain.at[3], 3)
+    told(4)
     def z_copy(k):
         return pltpu.make_async_remote_copy(src_ref=ap, dst_ref=AZ.at[zc], send_sem=z_send, recv_sem=z_recv, device_id=zring(k), device_id_type=MESH)
     with scope('z_send'):
@@ -643,12 +680,15 @@
             z_copy(k).start()
             z_copy(-k).start()
         z_copy(ZR // 2).start()
-    stores = [pltpu.make_async_copy(a, b, out_sem.at[k]) for k, (a, b) in enumerate(((XS, z_out), (B, b_out), (R1, r_out)))]
-    for c in stores:
-        c.start()
     def most(buf, send, recv):
         return pltpu.make_async_remote_copy(src_ref=buf.at[pl.ds(0, 31)], dst_ref=buf.at[pl.ds(0, 31)], send_sem=send, recv_sem=recv,
                                             device_id=at(1, 0), device_id_type=MESH)
+    landed(KS, len(near), ks_send, ks_recv).wait_send()
+    landed(KS, len(far), kf_send, kf_recv).wait_send()
+    for cyc in range(2):
+        landed(U.at[cyc], U_TILES, u_send, u_recv.at[cyc]).wait_send()
+    whole(FS, f_send, f_recv.at[0]).wait_send()
+    whole(SC, c_send, c_recv).wait_send()
     with scope('z_wait'):
         most(AZ, z_send, z_recv).wait_recv()
     part = AZ[0]
@@ -671,23 +711,12 @@
     ww = bb - 2.0 * br + rr
     coef = (bb - br) / ww
     size = jnp.sqrt((bb * rr - br * br) / (ww * bb))
-    scal[...] = jnp.where(ln == 0, coef, size)
-    for c in stores:
-        c.wait()
+    coef_out[...] = jnp.broadcast_to(coef, (1, 128))
+    rel_out[...] = jnp.broadcast_to(size, (1, 128))
 
     with scope('send_waits'):
         most(AP, p_send, p_recv).wait_send()
     most(AZ, z_send, z_recv).wait_send()
-    landed(KS, len(near), ks_send, ks_recv).wait_send()
-    landed(KS, len(far), kf_send, kf_recv).wait_send()
-    for cyc in range(2):
-        landed(U.at[cyc], NC - 1, u_send.at[cyc], u_recv.at[cyc]).wait_send()
-    for rnd in range(ROUNDS):
-        for c in face_copies(rnd):
-            c.wait_send()
-
-
-RSEM = [1, 0, 3, 2, 7, 6, 5, 4]
 
 
 def solution(mesh):
@@ -698,33 +727,34 @@
     scratch = [
         pltpu.VMEM((len(NAMES), 8, 128), f32), fine, pltpu.VMEM((1, 16), f32), pltpu.VMEM((1, 16), f32), pltpu.VMEM((64, 128), f32),
         pltpu.VMEM((2, 128), f32), pltpu.VMEM((NC, 2, 128), f32),
-        pltpu.VMEM((ROUNDS, 2, 8, 128), f32), pltpu.VMEM((ROUNDS, 2, 8, 128), f32), pltpu.VMEM((ROUNDS, 4, 1, 128), f32),
-        pltpu.VMEM((ROUNDS, 2, 8, 128), f32), pltpu.VMEM((ROUNDS, 2, 8, 128), f32), pltpu.VMEM((ROUNDS, 4, 1, 128), f32),
-        fine, fine, fine, fine, fine, fine,
+        pltpu.VMEM((ROUNDS, 4, 8, 128), f32), pltpu.VMEM((4, 1, 128), f32),
+        pltpu.VMEM((ROUNDS, 4, 8, 128), f32), pltpu.VMEM((4, 1, 128), f32),
+        fine, fine, fine,
         pltpu.VMEM((2, 8, 128), f32), pltpu.VMEM((2, NC, 8, 128), f32),
         col, col, col, col, col, col, col, col, col, col, col, col, col, col, pltpu.VMEM((9, 40, 128), f32),
         row, pltpu.VMEM((32, 1, 128), f32), row, pltpu.VMEM((32, 1, 128), f32),
-        pltpu.SemaphoreType.DMA((4,)), pltpu.SemaphoreType.DMA((3,)),
+        pltpu.SemaphoreType.DMA((4,)),
         pltpu.SemaphoreType.DMA, pltpu.SemaphoreType.DMA, pltpu.SemaphoreType.DMA, pltpu.SemaphoreType.DMA,
-        pltpu.SemaphoreType.DMA((ROUNDS, 8)), pltpu.SemaphoreType.DMA((ROUNDS, 8)),
-        pltpu.SemaphoreType.DMA((2,)), pltpu.SemaphoreType.DMA((2,)),
+        pltpu.SemaphoreType.DMA, pltpu.SemaphoreType.DMA,
+        pltpu.SemaphoreType.DMA, pltpu.SemaphoreType.DMA((ROUNDS,)),
+        pltpu.SemaphoreType.DMA, pltpu.SemaphoreType.DMA((2,)),
         pltpu.SemaphoreType.DMA, pltpu.SemaphoreType.DMA, pltpu.SemaphoreType.DMA, pltpu.SemaphoreType.DMA,
-        pltpu.SemaphoreType.REGULAR((4,)),
+        pltpu.SemaphoreType.REGULAR((7,)),
     ]
     hbm = pl.BlockSpec(memory_space=pl.ANY)
     call = pl.pallas_call(
         kernel,
-        out_shape=[jax.ShapeDtypeStruct((8, 8, 128), f32)] * 3 + [jax.ShapeDtypeStruct((1, 128), f32)],
+        out_shape=[pltpu.VMEM((8, 8, 128), f32)] * 3 + [pltpu.VMEM((1, 128), f32), pltpu.VMEM((1, 128), f32)],
         in_specs=[hbm] * 4,
-        out_specs=[hbm] * 3 + [pl.BlockSpec(memory_space=pltpu.VMEM)],
+        out_specs=[pl.BlockSpec(memory_space=pltpu.VMEM)] * 5,
         scratch_shapes=scratch,
         compiler_params=pltpu.CompilerParams(collective_id=0, has_side_effects=True),
         name="helmholtz",
     )
     def local(forcing, kappa, sigma):
-        z, b, r, scal = call(jnp.asarray(TABLE), forcing, kappa.reshape(1, 16), sigma.reshape(1, 16))
-        coef = scal[0, 0]
-        return coef * z, b - coef * (b - r), scal[0, 1]
+        z, b, r, coef, rel = call(jnp.asarray(TABLE), forcing, kappa.reshape(1, 16), sigma.reshape(1, 16))
+        coef = coef[None]
+        return coef * z, b - coef * (b - r), rel[0, 0]
 
     return jax.shard_map(local, mesh=mesh, in_specs=(P("gx", "gy", None),) * 3,
                          out_specs=(P("gx", "gy", None), P("gx", "gy", None), P()), check_vma=False)

time: 87.6 us -> 78.7 us (0.90)
  Pallas kernels: 83.4 us -> 76.1 us
  other arithmetic: 2.05 us -> 0.64 us
  local copies, waits for them, and re-layouts: 1.23 us -> 0 us
  between operations: 0.65 us -> 1.8 us
    pallas_call x1, Pallas kernels: 83.4 us -> 76.1 us  [local(): call(jnp.asarray(TABLE), forcing, kappa.reshape(1, 16), sigma.reshape(1,...]
    sub x1, other arithmetic: 2.05 us -> 0.64 us  [local(): return (coef * z, b - coef * (b - r), rel[0, 0])]
where the time goes in v3:
time: 78.7 us; the launch traced here: 78.5 us
  Pallas kernels  76.1 us (97%)
  between operations  1.8 us (2%)
    pallas_call x1, Pallas kernels, local(): call(jnp.asarray(TABLE), forcing, kappa.reshape(1, 16), sigma.reshape(1,...  76.1 us

profile of v3, /device:TPU:1, one launch (start us, length us, event | category | flops | bytes accessed | tf_op | source)
XLA Modules:
  0.0 78.5 jit_solution(9204332551055468332)
XLA Ops:
  0.6 76.1 %helmholtz.1 = (f32[8,8,128]{2,1,0:T(8,128)S(1)}, f32[8,8,128]{2,1,0:T(8,128)S(1)}, f32[8,8,128]{2,1,0:T(8,128)S(1)}, f32[1,128]{1,0:T(1,128)S(1)}, f32[1,128]{1,0:T(1,128)S(1)}) custom-call(f32[212,8,128]{2,1,0:T(8,128)} %constant.2.clone.tab_hbm, f32[8,8,128]{2,1,0:T(8,128)} %forc_hbm.1, f32[1,16]{1,0:T(1,128)} %bitcast.7, f32[1,16]{1,0:T(1,128)} %bitcast.8), custom_call_target="tpu_custom_call" | custom-call | tf_op jit(solution)/shard_map/helmholtz/pallas_call | solution.py:755
  76.7 0.6 multiply_subtract_fusion

commit v4 on v3

--- a/solution.py
+++ b/solution.py
@@ -134,6 +134,15 @@
         put(f"fo{i0}{j0}", ((i4 == a0) & (jp == b0 // 2)) * ones)
 for q in range(2): put(f"hot{q}", (lane // 8 == sub + 8 * q) * 1.0)
 NZ_ = lambda n: np.any(T[n] != 0)
+def z_matrix(tag, skip0):
+    m = np.zeros((128, 128), np.float32)
+    for d in range(-3, 4):
+        if d or not skip0:
+            for l in range(128): m[(l - 2 * d) % 128, l] += T[f"{tag}z{d}"][0, l]
+    return m
+ZM = {"a": z_matrix("a", True), "r": z_matrix("r", False), "p": z_matrix("p", False)}
+ZM["q"] = ZM["p"] @ ZM["a"]
+ZK = list(ZM)
 THETA, DELTA = 1.65, 1.35
 S_ = THETA / DELTA; rho0 = 1 / S_; rho1 = 1 / (2 * S_ - rho0)
 ALPHA = rho1 * rho0; BETA = 2 * rho1 / DELTA
@@ -141,6 +150,9 @@
 NAMES = [n for n in T if np.any(T[n])]
 INDEX = {n: k for k, n in enumerate(NAMES)}
 TABLE = np.stack([T[n] for n in NAMES])
+_H = [m.astype(jnp.bfloat16) for m in ZM.values()]
+_L = [(m - np.asarray(h, np.float32)).astype(jnp.bfloat16) for m, h in zip(ZM.values(), _H)]
+ZTABLE = np.stack([np.tile(np.concatenate([h, l], axis=1), (2, 1)) for h, l in zip(_H, _L)])
 K8 = [[float(np.float32(x)) for x in r] for r in K8]
 w8 = [float(np.float32(x)) for x in w8]
 
@@ -194,16 +206,14 @@
     same = pair(f"{tag}ya", f"{tag}yb")
     return same if out is None else (out if same is None else out + same)
 
-def a1(C, v, kap, sig):
-    k = C("a0") * v + xops(C, "a", v, True) + yops(C, "a", v, True) + zops(C, "a", v, True)
+def a1(C, v, kap, sig, z):
+    k = C("a0") * v + xops(C, "a", v, True) + yops(C, "a", v, True) + z
     return C("W1") * (kap * k + sig * v)
 
-def a2(C, v, kap, sig):
+def a2(C, v, kap, sig, z=None):
     k = xops(C, "b", v) + yops(C, "b", v) + zops(C, "b", v)
     return C("W2") * (kap * k + sig * v)
 
-def restrict2(C, v): return zops(C, "r", yops(C, "r", xops(C, "r", v)))
-def prolong2(C, v): return xops(C, "p", yops(C, "p", zops(C, "p", v)))
 def sz1(C, v): return v + C("z0") * lr(v, 2) + C("z3") * lr(v, -2)
 def xfrom_l(C, v): return C("x0") * sr(v, 2)
 def xfrom_r(C, v): return C("x3") * sr(v, -2)
@@ -246,7 +256,6 @@
 PARTNERS = [(dx, dy) for far in range(R, -1, -1) for dy in (2, 1, 3, 0) for dx in ((-far, far) if far else (0,)) if (dx, dy) != (0, 0)]
 ROUNDS = 7
 TI = 1.0 / THETA
-NEAR = 3
 EDGE = (-R, R)
 EDGE_ROWS = {R: (6, 2), -R: (0, 2)}
 U_TILES = NC - 1 - 2 * NY + 2 * NY // 4
@@ -256,9 +265,9 @@
     return (dx + R) * NY + dy % NY
 
 
-def kernel(tab_hbm, forc_hbm, kap_hbm, sig_hbm, XS, B, R1, coef_out, rel_out,
-           tab, forc, kap_in, sig_in, V, ks_s, KS, FS, SC, FR, RC, ID0, D0, Q,
-           us, U, ID1, ID2, C1B, D0B, VA, R1B, D1B, VB, C2B, G0B, QB, VC, X1, TMP, Z,
+def kernel(tab_hbm, zm_hbm, forc_hbm, kap_hbm, sig_hbm, XS, B, R1, coef_out, rel_out,
+           tab, zm, forc, kap_in, sig_in, V, ks_s, KS, FS, SC, FR, RC, ID0, D0, Q,
+           us, U, ID1, ID2, C1B, D0B, VA, R1B, D1B, VB, C2B, G0B, QB, VC, X1, TMP, ZD, Z,
            ap, AZ, pp, AP,
            in_sem, ks_send, kf_send, kf_recv, ks_recv, c_send, c_recv, f_send, f_recv, u_send, u_recv,
            z_send, z_recv, p_send, p_recv, chain):
@@ -283,7 +292,7 @@
     def C(name):
         return tab[INDEX[name]]
 
-    loads = [pltpu.make_async_copy(a, b, in_sem.at[k]) for k, (a, b) in enumerate(((kap_hbm, kap_in), (sig_hbm, sig_in), (tab_hbm, tab), (forc_hbm, forc)))]
+    loads = [pltpu.make_async_copy(a, b, in_sem.at[k]) for k, (a, b) in enumerate(((kap_hbm, kap_in), (sig_hbm, sig_in), (tab_hbm, tab), (forc_hbm, forc), (zm_hbm, zm)))]
     for c in loads:
         c.start()
     for cyc in range(2):
@@ -291,7 +300,7 @@
             for dy in range(NY):
                 U[cyc, slot(dx, dy)] = jnp.zeros((8, 128), jnp.float32)
     barrier = pltpu.get_barrier_semaphore()
-    greet = [at(dx, dy) for dx, dy in PARTNERS if abs(dx) <= NEAR]
+    greet = [at(-3, 0), at(3, 0), at(-2, 0), at(2, 0)] + [at(dx, dy) for dx, dy in PARTNERS if abs(dx) <= 1 and dy != 2]
     greet += [zring(-1), zring(1), plane(1, 0, 0), plane(3, 0, 0)]
     for d in greet:
         pl.semaphore_signal(barrier, inc=1, device_id=d, device_id_type=MESH)
@@ -325,32 +334,38 @@
         for i in range(8):
             V[8 * i:8 * i + 8] = tiles[i]
 
-    def face_start(rnd, to_x, to_y):
+    sublane = lax.broadcasted_iota(jnp.int32, (8, 128), 0)
+
+    def face_start(rnd, tiles, to_x, to_y):
+        keep(tiles)
         for s in range(2):
-            FS[rnd, s] = to_x[s]
-            FS[rnd, 2 + s] = V[pl.ds(7 * s, 8, stride=8)]
+            FS[rnd, s] = sz8(C, to_x[s])
+            rows = V[pl.ds(7 * s, 8, stride=8)]
             if to_y is not None:
-                FS[rnd, 2 + s, 0:1] = to_y[0][7 * s:7 * s + 1]
-                FS[rnd, 2 + s, 7:8] = to_y[1][7 * s:7 * s + 1]
+                a, b = (to_y[0], sr(to_y[1], 7)) if s == 0 else (sr(to_y[0], 1), to_y[1])
+                rows = jnp.where(sublane == 0, a, jnp.where(sublane == 7, b, rows))
+            FS[rnd, 2 + s] = sz8(C, rows)
         with scope('face_start'):
             for c in side_copies(rnd):
                 c.start()
+        keep([sz8(C, t) for t in tiles])
 
     def face_wait(rnd, corners=False):
         with scope('face_wait'):
             whole(FR.at[rnd], f_send, f_recv.at[rnd]).wait_recv()
             if corners:
                 whole(RC, c_send, c_recv).wait_recv()
-        V[0:8] = V[0:8] + FR[rnd, 0]
-        V[56:64] = V[56:64] + FR[rnd, 1]
-        for s in range(2):
-            V[pl.ds(7 * s, 8, stride=8)] = V[pl.ds(7 * s, 8, stride=8)] + FR[rnd, 2 + s]
-        if corners:
-            for k, r in enumerate((0, 7, 56, 63)):
-                V[r:r + 1] = V[r:r + 1] + RC[k]
-        return [V[8 * i:8 * i + 8] for i in range(8)]
-
-    first_v = [sz8(C, forc[i]) for i in range(8)]
+        out = []
+        for i in range(8):
+            t = V[8 * i:8 * i + 8] + C("jm0") * FR[rnd, 2, i:i + 1] + C("jm7") * FR[rnd, 3, i:i + 1]
+            if i in (0, 7):
+                t = t + FR[rnd, i // 7]
+                if corners:
+                    t = t + C("jm0") * RC[2 * (i // 7)] + C("jm7") * RC[2 * (i // 7) + 1]
+            out.append(t)
+        return out
+
+    first_v = [forc[i] for i in range(8)]
     with scope('barrier'):
         pl.semaphore_wait(barrier, len(greet))
 
@@ -360,14 +375,20 @@
                                             recv_sem=ks_recv if near else kf_recv, device_id=at(dx, dy), device_id_type=MESH)
     near = [(dx, dy) for dx, dy in PARTNERS if abs(dx) <= 1 and dy != 2]
     far = [p for p in PARTNERS if p not in near]
-    for p in near:
-        ks_copy(*p).start()
-    keep(first_v)
-    for k, r in enumerate((0, 7, 56, 63)):
-        SC[k] = V[r:r + 1]
+    far1 = [p for p in far if abs(p[0]) <= (2 if p[1] == 2 else 4) or p[1] == 0]
+    far2 = [p for p in far if p not in far1]
+
+    def ks_to(group):
+        with scope('ks_send'):
+            for p in group:
+                ks_copy(*p).start()
+
+    ks_to(near)
+    for k, (i, r) in enumerate(((0, 0), (0, 7), (7, 0), (7, 7))):
+        SC[k] = sz8(C, first_v[i])[r:r + 1]
     for c in corner_copies():
         c.start()
-    face_start(0, (first_v[0], first_v[7]), None)
+    face_start(0, first_v, (first_v[0], first_v[7]), None)
     def tell(n, to):
         for d in to:
             pl.semaphore_signal(chain.at[n], inc=1, device_id=d, device_id_type=MESH)
@@ -375,7 +396,7 @@
     def told(n, count=2):
         pl.semaphore_wait(chain.at[n], count)
 
-    tell(0, (at(-NEAR, 0), at(NEAR, 0)))
+    tell(0, (at(-3, 0), at(3, 0)))
     tell(1, (zring(-1), zring(1)))
     tell(5, (plane(1, 0, 0), plane(3, 0, 0)))
 
@@ -403,13 +424,8 @@
 
     b = face_wait(0, True)
     told(0)
-    with scope('ks_send'):
-        for p in far:
-            ks_copy(*p).start()
-    told(1)
-    tell(2, (zring(-2), zring(2)))
-    told(5)
-    tell(6, (plane(2, 0, 0),))
+    tell(7, (at(-5, 0), at(5, 0)))
+    ks_to(far1)
     for i in range(8):
         B[i] = b[i]
         R1[i] = b[i]
@@ -473,9 +489,22 @@
             for dy in range(NY):
                 put((dx + R) * NY + dy, s[dy])
 
-    def image(op, src, dst, radius):
-        for dx, dy, c in columns(radius):
-            TMP[c] = op(C, src[c], kap_of(dx, dy), sig_of(dx, dy))
+    def along_z(src, radius, *tags):
+        lo, n = (R - radius) * NY, (2 * radius + 1) * NY
+        v = src[lo:lo + n].reshape(n * 8, 128)
+        high = v.astype(jnp.bfloat16)
+        low = (v - high.astype(jnp.float32)).astype(jnp.bfloat16)
+        both = jnp.concatenate([high, low], axis=1)
+        out = []
+        for tag in tags:
+            p = jnp.dot(both, zm[ZK.index(tag)], preferred_element_type=jnp.float32)
+            out.append((p[:, 0:128] + p[:, 128:256]).reshape(n, 8, 128))
+        return out
+
+    def image(op, src, dst, radius, tag=None):
+        z = along_z(src, radius, tag)[0] if tag else None
+        for n, (dx, dy, c) in enumerate(columns(radius)):
+            TMP[c] = op(C, src[c], kap_of(dx, dy), sig_of(dx, dy), z[n] if tag else None)
         for dx, dy, c in columns(radius):
             dst[c] = sz1(C, TMP[c])
 
@@ -494,27 +523,32 @@
             QB[c] = (1.0 + ALPHA) * G0B[c] + BETA * (C2B[c] - s) * ID2[c]
         with scope('first'):
             sums(U.at[cyc], R - 1, put1)
-            image(a1, D0B, VA, R - 1)
+            image(a1, D0B, VA, R - 1, 'a')
         with scope('second'):
             sums(VA, R - 2, put2)
-            for dx, dy, c in columns(R - 2):
-                TMP[c] = C("m1") * R1B[c] - a1(C, D1B[c], kap_of(dx, dy), sig_of(dx, dy))
+            z, = along_z(D1B, R - 2, "a")
+            for n, (dx, dy, c) in enumerate(columns(R - 2)):
+                TMP[c] = C("m1") * R1B[c] - a1(C, D1B[c], kap_of(dx, dy), sig_of(dx, dy), z[n])
+                if abs(dx) <= R - 4:
+                    ZD[c] = z[n]
             for dx, dy, c in columns(R - 2):
                 TMP[c] = yops(C, "r", xops(C, "r", TMP[c]))
-            for dx, dy, c in columns(R - 2):
-                TMP[c] = zops(C, "r", TMP[c])
-            for dx, dy, c in columns(R - 2):
-                VB[c] = sz1(C, TMP[c])
+            z, = along_z(TMP, R - 2, "r")
+            for n, (dx, dy, c) in enumerate(columns(R - 2)):
+                VB[c] = sz1(C, z[n])
         with scope('third'):
             sums(VB, R - 3, put3)
             image(a2, G0B, VA, R - 3)
         with scope('fourth'):
             sums(VA, R - 4, put4)
+            zp, zq = along_z(QB, R - 4, "p", "q")
+            for n, (dx, dy, c) in enumerate(columns(R - 4)):
+                q = D1B[c] + xops(C, "p", yops(C, "p", zp[n]))
+                z = ZD[c] + xops(C, "p", yops(C, "p", zq[n]))
+                QB[c] = q
+                TMP[c] = a1(C, q, kap_of(dx, dy), sig_of(dx, dy), z)
             for dx, dy, c in columns(R - 4):
-                TMP[c] = zops(C, "p", QB[c])
-            for dx, dy, c in columns(R - 4):
-                QB[c] = D1B[c] + xops(C, "p", yops(C, "p", TMP[c]))
-            image(a1, QB, VC, R - 4)
+                VC[c] = sz1(C, TMP[c])
         with scope('fifth'):
             def put5(c, s):
                 X1[c] = D0B[c] + QB[c] + TI * (R1B[c] - s) * ID1[c]
@@ -598,14 +632,7 @@
         return e
 
     def image_start(rnd, v):
-        out, to_x, to_y = a_fine(C, v, kap, sig, sides)
-        keep([sz8(C, t) for t in out])
-        face_start(rnd, [sz8(C, t) for t in to_x], [sz8(C, t) for t in to_y])
-        return out
-
-    def apply(rnd, v):
-        image_start(rnd, v)
-        return face_wait(rnd)
+        face_start(rnd, *a_fine(C, v, kap, sig, sides))
 
     def cycle(cyc, carry):
         rnd = 1 + 3 * cyc
@@ -613,7 +640,16 @@
         d0 = [TI * r[i] * ID0[i] for i in range(8)]
         for i in range(8):
             D0[i] = d0[i]
-        s = apply(rnd, d0)
+        image_start(rnd, d0)
+        @pl.when(cyc == 0)
+        def _():
+            told(1)
+            tell(2, (zring(-2), zring(2)))
+            told(5)
+            tell(6, (plane(2, 0, 0),))
+            told(7)
+            ks_to(far2)
+        s = face_wait(rnd)
         d1, t = [], []
         for i in range(8):
             r1 = R1[i] - s[i]
@@ -628,13 +664,12 @@
         with scope('u_send'):
             for dx, dy in PARTNERS:
                 u_copy(cyc, dx, dy).start()
-        keep([sz8(C, p) for p in w])
-        face_start(rnd + 1, [sz8(C, p) for p in to_x], [sz8(C, p) for p in to_y])
+        face_start(rnd + 1, w, to_x, to_y)
         @pl.when(cyc == 0)
         def _():
-            coarse_diagonals()
             told(2)
             tell(3, (zring(-4), zring(4)))
+            coarse_diagonals()
             told(6, 1)
         s = face_wait(rnd + 1)
         for i in range(8):
@@ -642,10 +677,6 @@
         with scope('u_wait'):
             landed(U.at[cyc], U_TILES, u_send, u_recv.at[cyc]).wait_recv()
         coarse(cyc)
-        @pl.when(cyc == 0)
-        def _():
-            told(3)
-            tell(4, (zring(-8), zring(8)))
         with scope('corr'):
             e = correction()
         for i in range(8):
@@ -658,7 +689,12 @@
             x = TI * r3 * ID0[i]
             dl.append(x)
             XS[i] = XS[i] + (D0[i] + Q[i] + x)
-        s = apply(rnd + 2, dl)
+        image_start(rnd + 2, dl)
+        s = face_wait(rnd + 2)
+        @pl.when(cyc == 0)
+        def _():
+            told(3)
+            tell(4, (zring(-8), zring(8)))
         for i in range(8):
             R1[i] = R1[i] - s[i]
         return carry
@@ -725,36 +761,36 @@
     fine = pltpu.VMEM((8, 8, 128), f32)
     row = pltpu.VMEM((1, 128), f32)
     scratch = [
-        pltpu.VMEM((len(NAMES), 8, 128), f32), fine, pltpu.VMEM((1, 16), f32), pltpu.VMEM((1, 16), f32), pltpu.VMEM((64, 128), f32),
+        pltpu.VMEM((len(NAMES), 8, 128), f32), pltpu.VMEM((len(ZK), 256, 256), jnp.bfloat16), fine, pltpu.VMEM((1, 16), f32), pltpu.VMEM((1, 16), f32), pltpu.VMEM((64, 128), f32),
         pltpu.VMEM((2, 128), f32), pltpu.VMEM((NC, 2, 128), f32),
         pltpu.VMEM((ROUNDS, 4, 8, 128), f32), pltpu.VMEM((4, 1, 128), f32),
         pltpu.VMEM((ROUNDS, 4, 8, 128), f32), pltpu.VMEM((4, 1, 128), f32),
         fine, fine, fine,
         pltpu.VMEM((2, 8, 128), f32), pltpu.VMEM((2, NC, 8, 128), f32),
-        col, col, col, col, col, col, col, col, col, col, col, col, col, col, pltpu.VMEM((9, 40, 128), f32),
+        col, col, col, col, col, col, col, col, col, col, col, col, col, col, col, pltpu.VMEM((9, 40, 128), f32),
         row, pltpu.VMEM((32, 1, 128), f32), row, pltpu.VMEM((32, 1, 128), f32),
-        pltpu.SemaphoreType.DMA((4,)),
+        pltpu.SemaphoreType.DMA((5,)),
         pltpu.SemaphoreType.DMA, pltpu.SemaphoreType.DMA, pltpu.SemaphoreType.DMA, pltpu.SemaphoreType.DMA,
         pltpu.SemaphoreType.DMA, pltpu.SemaphoreType.DMA,
         pltpu.SemaphoreType.DMA, pltpu.SemaphoreType.DMA((ROUNDS,)),
         pltpu.SemaphoreType.DMA, pltpu.SemaphoreType.DMA((2,)),
         pltpu.SemaphoreType.DMA, pltpu.SemaphoreType.DMA, pltpu.SemaphoreType.DMA, pltpu.SemaphoreType.DMA,
-        pltpu.SemaphoreType.REGULAR((7,)),
+        pltpu.SemaphoreType.REGULAR((8,)),
     ]
     hbm = pl.BlockSpec(memory_space=pl.ANY)
     call = pl.pallas_call(
         kernel,
         out_shape=[pltpu.VMEM((8, 8, 128), f32)] * 3 + [pltpu.VMEM((1, 128), f32), pltpu.VMEM((1, 128), f32)],
-        in_specs=[hbm] * 4,
+        in_specs=[hbm] * 5,
         out_specs=[pl.BlockSpec(memory_space=pltpu.VMEM)] * 5,
         scratch_shapes=scratch,
         compiler_params=pltpu.CompilerParams(collective_id=0, has_side_effects=True),
         name="helmholtz",
     )
     def local(forcing, kappa, sigma):
-        z, b, r, coef, rel = call(jnp.asarray(TABLE), forcing, kappa.reshape(1, 16), sigma.reshape(1, 16))
+        z, b, r, coef, rel = call(jnp.asarray(TABLE), jnp.asarray(ZTABLE), forcing, kappa.reshape(1, 16), sigma.reshape(1, 16))
         coef = coef[None]
-        return coef * z, b - coef * (b - r), rel[0, 0]
+        return coef * z, b - coef * (b - r), rel[0, 1]
 
     return jax.shard_map(local, mesh=mesh, in_specs=(P("gx", "gy", None),) * 3,
                          out_specs=(P("gx", "gy", None), P("gx", "gy", None), P()), check_vma=False)

time: 78.7 us -> 76.4 us (0.971)
  Pallas kernels: 76.1 us -> 74.4 us
  between operations: 1.8 us -> 0.64 us
    pallas_call x1, Pallas kernels: 76.1 us -> 74.4 us  [local(): call(jnp.asarray(TABLE), jnp.asarray(ZTABLE), forcing, kappa.reshape(1, 1...]
where the time goes in v4:
time: 76.4 us; the launch traced here: 76.3 us
  Pallas kernels  74.4 us (97%)
    pallas_call x1, Pallas kernels, local(): call(jnp.asarray(TABLE), jnp.asarray(ZTABLE), forcing, kappa.reshape(1, 1...  74.4 us

profile of v4, /device:TPU:1, one launch (start us, length us, event | category | flops | bytes accessed | tf_op | source)
XLA Modules:
  0.0 76.3 jit_solution(12378158880058999465)
XLA Ops:
  0.6 74.4 %helmholtz.1 = (f32[8,8,128]{2,1,0:T(8,128)S(1)}, f32[8,8,128]{2,1,0:T(8,128)S(1)}, f32[8,8,128]{2,1,0:T(8,128)S(1)}, f32[1,128]{1,0:T(1,128)S(1)}, f32[1,128]{1,0:T(1,128)S(1)}) custom-call(f32[212,8,128]{2,1,0:T(8,128)} %constant.4.clone.tab_hbm, bf16[4,256,256]{2,1,0:T(8,128)(2,1)} %constant.5.clone.zm_hbm, f32[8,8,128]{2,1,0:T(8,128)} %forc_hbm.1, ...), custom_call_target="tpu_custom_call" | custom-call | tf_op jit(solution)/shard_map/helmholtz/pallas_call | solution.py:791
  75.0 0.6 slice.3
  75.6 0.6 multiply_subtract_fusion
